TPU v7x, 64 devices: a 2x2x8 block of a 4x4x8 slice. The times are simulated.
64 devices in a mesh: dp: 4 (over x, y), cp: 16 (over z, core).
Axes of the slice: x: 2, y: 2, z: 8, core: 2. Of those that a mesh axis runs over, the one named last changes fastest.
The devices are a block of a 4x4x8 slice.
Arguments:
- q_rope: bfloat16 [4, 8192, 40, 128], P('dp', 'cp'), parts along dimension 0
- k_rope: bfloat16 [4, 8192, 8, 128], P('dp', 'cp'), parts along dimension 0
- values: bfloat16 [4, 8192, 8, 128], P('dp', 'cp'), parts along dimension 0
- d_out: bfloat16 [4, 8192, 40, 128], P('dp', 'cp'), parts along dimension 0
Outputs:
- output 1: bfloat16 [4, 8192, 40, 128], P('dp', 'cp'), parts along dimension 0
- output 2: bfloat16 [4, 8192, 40, 128], P('dp', 'cp'), parts along dimension 0
- output 3: bfloat16 [4, 8192, 8, 128], P('dp', 'cp'), parts along dimension 0
- output 4: bfloat16 [4, 8192, 8, 128], P('dp', 'cp'), parts along dimension 0
There are 4 independent parts. A program takes and returns all parts, laid end to end along the dimension named above; each array names one.
All inputs are finite; a program needn't handle non-finite values.
Results may differ from a plain program's by a relative error of at most 0.00808623.
Values are sent between devices in bfloat16 or wider.
A program may use at most 768 MiB of HBM per device.

v0:
```python
import jax
import jax.numpy as jnp
from jax import lax
from jax.sharding import PartitionSpec as P

BLOCK = 64
LOCAL = 16
STRIDE = 8


def residue_table(kv_heads, group_size):
    head_ids = jnp.arange(kv_heads)[:, None] * group_size + jnp.arange(group_size)[None, :]
    return (-1 - head_ids) % STRIDE


def select_matrix(kv_heads, group_size):
    residues = residue_table(kv_heads, group_size)
    return (jnp.arange(STRIDE)[None, None, :] == residues[:, :, None]).astype(jnp.bfloat16)


def compact(keys_in, group_size):
    n_batch, seq_len, kv_heads, head_dim = keys_in.shape
    grouped = keys_in.reshape(n_batch, seq_len // (BLOCK * STRIDE), STRIDE, BLOCK, kv_heads, head_dim)
    picked = jnp.einsum('bmsigd,gus->bmigud', grouped, select_matrix(kv_heads, group_size), preferred_element_type=jnp.float32)
    return picked.astype(jnp.bfloat16).reshape(n_batch, seq_len // STRIDE, kv_heads, group_size, head_dim)


def expand(grads, group_size):
    n_batch, str_len, kv_heads = grads.shape[0], grads.shape[1], grads.shape[2]
    head_dim = grads.shape[4]
    grouped = grads.reshape(n_batch, str_len // BLOCK, BLOCK, kv_heads, group_size, head_dim)
    spread = jnp.einsum('bmigud,gus->bmsigd', grouped, select_matrix(kv_heads, group_size).astype(jnp.float32))
    return spread.reshape(n_batch, str_len * STRIDE, kv_heads, head_dim)


def shard_attention(q_rope, d_out, k_ext, v_ext, k_str, v_str, shard_idx):
    n_batch, seq_loc, heads, head_dim = q_rope.shape
    kv_heads = k_ext.shape[2]
    group_size = heads // kv_heads
    n_blocks = seq_loc // BLOCK
    halo = (LOCAL - 1) * BLOCK
    window = LOCAL * BLOCK
    scale = 1.0 / head_dim
    str_block = (jnp.arange(k_str.shape[1]) // BLOCK)[None, None, :] * STRIDE + residue_table(kv_heads, group_size)[:, :, None]
    row_ids = jnp.arange(BLOCK)[:, None]
    col_ids = jnp.arange(window)[None, :]
    blk_shape = (n_batch, BLOCK, kv_heads, group_size, head_dim)

    def body(carry, blk_idx):
        dk_ext, dv_ext, dk_str, dv_str = carry
        win_start = blk_idx * BLOCK
        q_blk = lax.dynamic_slice_in_dim(q_rope, win_start, BLOCK, axis=1).reshape(blk_shape)
        do_blk = lax.dynamic_slice_in_dim(d_out, win_start, BLOCK, axis=1).reshape(blk_shape)
        k_win = lax.dynamic_slice_in_dim(k_ext, win_start, window, axis=1)
        v_win = lax.dynamic_slice_in_dim(v_ext, win_start, window, axis=1)
        q_global = shard_idx * n_blocks + blk_idx
        loc_mask = (col_ids <= row_ids + halo) & (col_ids >= halo - q_global * BLOCK)
        str_mask = (str_block <= q_global - LOCAL)[:, :, None, :]
        s_loc = jnp.einsum('bigud,bjgd->bguij', q_blk, k_win, preferred_element_type=jnp.float32) * scale
        s_str = jnp.einsum('bigud,bjgud->bguij', q_blk, k_str, preferred_element_type=jnp.float32) * scale
        s_loc = jnp.where(loc_mask, s_loc, -jnp.inf)
        s_str = jnp.where(str_mask, s_str, -jnp.inf)
        row_max = jnp.maximum(jnp.max(s_loc, axis=-1), jnp.max(s_str, axis=-1))[..., None]
        e_loc = jnp.exp(s_loc - row_max)
        e_str = jnp.exp(s_str - row_max)
        row_sum = jnp.sum(e_loc, axis=-1, keepdims=True) + jnp.sum(e_str, axis=-1, keepdims=True)
        p_loc = e_loc / row_sum
        p_str = e_str / row_sum
        pb_loc = p_loc.astype(jnp.bfloat16)
        pb_str = p_str.astype(jnp.bfloat16)
        o_blk = (jnp.einsum('bguij,bjgd->bigud', pb_loc, v_win, preferred_element_type=jnp.float32)
                 + jnp.einsum('bguij,bjgud->bigud', pb_str, v_str, preferred_element_type=jnp.float32))
        row_delta = jnp.einsum('bigud,bigud->bgui', do_blk.astype(jnp.float32), o_blk)[..., None]
        dp_loc = jnp.einsum('bigud,bjgd->bguij', do_blk, v_win, preferred_element_type=jnp.float32)
        dp_str = jnp.einsum('bigud,bjgud->bguij', do_blk, v_str, preferred_element_type=jnp.float32)
        ds_loc = (p_loc * (dp_loc - row_delta)).astype(jnp.bfloat16)
        ds_str = (p_str * (dp_str - row_delta)).astype(jnp.bfloat16)
        dq_blk = (jnp.einsum('bguij,bjgd->bigud', ds_loc, k_win, preferred_element_type=jnp.float32)
                  + jnp.einsum('bguij,bjgud->bigud', ds_str, k_str, preferred_element_type=jnp.float32)) * scale
        dk_win = jnp.einsum('bguij,bigud->bjgd', ds_loc, q_blk, preferred_element_type=jnp.float32) * scale
        dv_win = jnp.einsum('bguij,bigud->bjgd', pb_loc, do_blk, preferred_element_type=jnp.float32)
        dk_ext = lax.dynamic_update_slice_in_dim(dk_ext, lax.dynamic_slice_in_dim(dk_ext, win_start, window, axis=1) + dk_win, win_start, axis=1)
        dv_ext = lax.dynamic_update_slice_in_dim(dv_ext, lax.dynamic_slice_in_dim(dv_ext, win_start, window, axis=1) + dv_win, win_start, axis=1)
        dk_str = dk_str + jnp.einsum('bguij,bigud->bjgud', ds_str, q_blk, preferred_element_type=jnp.float32) * scale
        dv_str = dv_str + jnp.einsum('bguij,bigud->bjgud', pb_str, do_blk, preferred_element_type=jnp.float32)
        return (dk_ext, dv_ext, dk_str, dv_str), (o_blk.astype(jnp.bfloat16), dq_blk.astype(jnp.bfloat16))

    init = (jnp.zeros(k_ext.shape, jnp.float32), jnp.zeros(v_ext.shape, jnp.float32), jnp.zeros(k_str.shape, jnp.float32), jnp.zeros(v_str.shape, jnp.float32))
    carry, stacked = lax.scan(body, init, jnp.arange(n_blocks))
    out_shape = (n_batch, seq_loc, heads, head_dim)
    attn_out = jnp.moveaxis(stacked[0], 0, 1).reshape(out_shape)
    d_q = jnp.moveaxis(stacked[1], 0, 1).reshape(out_shape)
    return (attn_out, d_q) + carry


def halo_lengths(seq_loc):
    halo = (LOCAL - 1) * BLOCK
    hop_count = -(-halo // seq_loc)
    return [seq_loc] * (hop_count - 1) + [halo - (hop_count - 1) * seq_loc]


def fetch_halo(local_part, lengths, cp_size):
    seq_loc = local_part.shape[1]
    pieces = []
    for dist in range(len(lengths), 0, -1):
        tail_part = local_part[:, seq_loc - lengths[dist - 1]:]
        if dist < cp_size:
            pieces.append(lax.ppermute(tail_part, 'cp', [(sender, sender + dist) for sender in range(cp_size - dist)]))
        else:
            pieces.append(jnp.zeros_like(tail_part))
    return jnp.concatenate(pieces + [local_part], axis=1)


def return_halo(halo_grad, lengths, cp_size, seq_loc):
    result = jnp.zeros(halo_grad.shape[:1] + (seq_loc,) + halo_grad.shape[2:], jnp.float32)
    offset = 0
    for dist in range(len(lengths), 0, -1):
        size_d = lengths[dist - 1]
        seg_part = halo_grad[:, offset:offset + size_d]
        offset = offset + size_d
        if dist < cp_size:
            arrived = lax.ppermute(seg_part.astype(jnp.bfloat16), 'cp', [(sender + dist, sender) for sender in range(cp_size - dist)])
            result = result + jnp.pad(arrived, ((0, 0), (seq_loc - size_d, 0), (0, 0), (0, 0))).astype(jnp.float32)
    return result


def owner_sum(contrib, cp_size):
    received = lax.all_to_all(contrib.astype(jnp.bfloat16), 'cp', 1, 1, tiled=True)
    split_shape = received.shape[:1] + (cp_size, received.shape[1] // cp_size) + received.shape[2:]
    return jnp.sum(received.reshape(split_shape), axis=1, dtype=jnp.float32)


def solution(mesh):
    cp_size = mesh.shape['cp']
    spec = P('dp', 'cp', None, None)

    def per_device(q_rope, k_rope, values, d_out):
        seq_loc = q_rope.shape[1]
        group_size = q_rope.shape[2] // k_rope.shape[2]
        halo = (LOCAL - 1) * BLOCK
        lengths = halo_lengths(seq_loc)
        shard_idx = lax.axis_index('cp')
        k_ext = fetch_halo(k_rope, lengths, cp_size)
        v_ext = fetch_halo(values, lengths, cp_size)
        k_str = lax.all_gather(compact(k_rope, group_size), 'cp', axis=1, tiled=True)
        v_str = lax.all_gather(compact(values, group_size), 'cp', axis=1, tiled=True)
        attn_out, d_q, dk_ext, dv_ext, dk_str, dv_str = shard_attention(q_rope, d_out, k_ext, v_ext, k_str, v_str, shard_idx)
        d_k = dk_ext[:, halo:] + return_halo(dk_ext[:, :halo], lengths, cp_size, seq_loc) + expand(owner_sum(dk_str, cp_size), group_size)
        d_v = dv_ext[:, halo:] + return_halo(dv_ext[:, :halo], lengths, cp_size, seq_loc) + expand(owner_sum(dv_str, cp_size), group_size)
        return attn_out, d_q, d_k.astype(jnp.bfloat16), d_v.astype(jnp.bfloat16)

    return jax.shard_map(per_device, mesh=mesh, in_specs=(spec, spec, spec, spec), out_specs=(spec, spec, spec, spec), check_vma=False)
```

profile of v0, /device:TPU:21, one launch (start us, length us, event | category | flops | bytes accessed | tf_op | source)
XLA Modules:
  0.0 2193.2 jit_solution(15287105283175395489)
XLA Ops:
  32.8 60.0 %collective-permute-done.2 = bf16[1,448,8,128]{3,1,2,0:T(8,128)(2,1)} collective-permute-done((bf16[1,448,8,128]{3,1,2,0:T(8,128)(2,1)}, bf16[1,448,8,128]{3,1,2,0:T(8,128)(2,1)}, u32[]{:S(2)}, u32[]{:S(2)}) %collective-permute-start.2) | collective-permute-done | bytes 917536 | tf_op jit(solution)/shard_map/ppermute | solution.py:108
  96.1 62.5 %collective-permute-done = bf16[1,448,8,128]{3,1,2,0:T(8,128)(2,1)} collective-permute-done((bf16[1,448,8,128]{3,1,2,0:T(8,128)(2,1)}, bf16[1,448,8,128]{3,1,2,0:T(8,128)(2,1)}, u32[]{:S(2)}, u32[]{:S(2)}) %collective-permute-start) | collective-permute-done | bytes 917536 | tf_op jit(solution)/shard_map/ppermute | solution.py:108
  161.7 12.4 copy.67
  174.1 86.2 %all-gather.5.cloned.1.call-done = bf16[1,1,1024,8,5,128]{5,4,2,3,1,0:T(8,128)(2,1)} async-done(((bf16[1,1,64,8,5,128]{5,4,2,3,1,0:T(8,128)(2,1)}), bf16[1,1,1024,8,5,128]{5,4,2,3,1,0:T(8,128)(2,1)}) %all-gather.5.cloned.1.call-update) | async-done | bytes 10485776 | tf_op jit(solution)/shard_map/all_gather | solution.py:145
  260.2 12.3 copy.65
  278.0 1338.1 %while.24 = (s32[]{:T(128)}, f32[1,1472,8,128]{3,2,1,0:T(8,128)}, f32[1,1472,8,128]{3,2,1,0:T(8,128)}, f32[1,1024,8,5,128]{1,4,3,2,0:T(8,128)}, f32[1,1024,8,5,1...) while((s32[]{:T(128)}, f32[1,1472,8,128]{3,2,1,0:T(8,128)}, ...), condition=%wide.region_5.6_spmd.clone.clone, body=%wide.region_0.5_spmd.clone.clone.sunk | while | flops 8211080704 | bytes 579921472 | solution.py:89
  322.9 12.3 fusion.185
  359.1 8.8 fusion.188
  390.7 7.3 constant_dynamic-update-slice_fusion.3
  399.0 14.6 multiply_convert_fusion.2
  413.7 7.7 fusion.191
  426.2 12.2 bitcast_add_fusion.11
  438.5 12.4 bitcast_add_fusion.10
  477.1 12.3 fusion.185
  513.4 8.8 fusion.188
  553.2 14.6 multiply_convert_fusion.2
  567.9 7.7 fusion.191
  580.4 18.4 bitcast_add_fusion.11
  598.8 18.4 bitcast_add_fusion.10
  643.5 12.3 fusion.185
  679.8 8.8 fusion.188
  719.7 14.6 multiply_convert_fusion.2
  734.3 7.7 fusion.191
  746.9 18.4 bitcast_add_fusion.11
  765.3 18.4 bitcast_add_fusion.10
  810.0 12.3 fusion.185
  846.3 8.8 fusion.188
  886.1 14.6 multiply_convert_fusion.2
  900.7 7.7 fusion.191
  913.3 18.4 bitcast_add_fusion.11
  931.7 18.4 bitcast_add_fusion.10
  976.4 12.3 fusion.185
  1012.7 8.8 fusion.188
  1052.4 14.6 multiply_convert_fusion.2
  1067.1 7.7 fusion.191
  1079.7 18.4 bitcast_add_fusion.11
  1098.1 18.4 bitcast_add_fusion.10
  1142.8 12.3 fusion.185
  1179.0 8.8 fusion.188
  1218.8 14.6 multiply_convert_fusion.2
  1233.5 7.7 fusion.191
  1246.1 18.4 bitcast_add_fusion.11
  1264.5 18.4 bitcast_add_fusion.10
  1309.2 12.3 fusion.185
  1345.4 8.8 fusion.188
  1377.0 7.4 constant_dynamic-update-slice_fusion.3
  1385.3 14.6 multiply_convert_fusion.2
  1400.0 7.7 fusion.191
  1412.5 18.4 bitcast_add_fusion.11
  1430.9 18.4 bitcast_add_fusion.10
  1475.6 12.3 fusion.185
  1511.9 8.8 fusion.188
  1543.5 7.3 constant_dynamic-update-slice_fusion.3
  1551.7 14.6 multiply_convert_fusion.2
  1566.4 7.7 fusion.191
  1579.0 18.4 bitcast_add_fusion.11
  1597.4 18.4 bitcast_add_fusion.10
  1616.1 19.2 copy.72
  1640.3 19.2 copy.78
  1659.5 217.6 %all-to-all-done = bf16[1,1024,8,5,128]{4,2,3,0,1:T(8,128)(2,1)} async-done(((bf16[1,1024,8,5,128]{4,2,3,0,1:T(8,128)(2,1)}), bf16[1,1024,8,5,128]{4,2,3,0,1:T(8,128)(2,1)}, u32[]{:S(2)}, u32[]{:S(2)}) %all-to-all-start) | async-done | bytes 10485792 | tf_op jit(solution)/shard_map/all_to_all | solution.py:128
  1918.0 203.7 %all-to-all-done.1 = bf16[1,1024,8,5,128]{4,2,3,0,1:T(8,128)(2,1)} async-done(((bf16[1,1024,8,5,128]{4,2,3,0,1:T(8,128)(2,1)}), bf16[1,1024,8,5,128]{4,2,3,0,1:T(8,128)(2,1)}, u32[]{:S(2)}, u32[]{:S(2)}) %all-to-all-start.1) | async-done | bytes 10485792 | tf_op jit(solution)/shard_map/all_to_all | solution.py:128
  2128.7 11.9 collective-permute-done.4
  2140.6 21.3 collective-permute-done.5
  2165.4 17.6 collective-permute-done.7
  (820 shorter events, 750.6 us)
Async XLA Ops:
  7.2 18.5 copy-start.18
  7.2 154.5 %all-gather.7.cloned.1.call-start = ((), (), s32[]{:S(2)}) async-start(), calls=%async_computation.3 | async-start | bytes 17825792 | tf_op jit(solution)/shard_map/all_gather | solution.py:146
  11.0 249.2 %all-gather.5.cloned.1.call-start = ((), (), s32[]{:S(2)}) async-start(), calls=%async_computation.2 | async-start | bytes 17825792 | tf_op jit(solution)/shard_map/all_gather | solution.py:145
  14.7 78.1 %collective-permute-start.3 = (bf16[1,512,8,128]{3,1,2,0:T(8,128)(2,1)S(1)}, bf16[1,512,8,128]{3,1,2,0:T(8,128)(2,1)}, u32[]{:S(2)}, u32[]{:S(2)}) collective-permute-start(bf16[1,512,8,128]{3,1,2,0:T(8,128)(2,1)S(1)} %copy.59), channel_id=1, source_target_pairs={{0,1},{1,2},{2,3},{3,4},{4,5},{5,6},{6,7},{7,8},{8,9},{9,10},{10,1... | collective-permute-start | bytes 3145736 | tf_op jit(solution)/shard_map/ppermute | solution.py:108
  20.9 71.9 %collective-permute-start.2 = (bf16[1,448,8,128]{3,1,2,0:T(8,128)(2,1)}, bf16[1,448,8,128]{3,1,2,0:T(8,128)(2,1)}, u32[]{:S(2)}, u32[]{:S(2)}) collective-permute-start(bf16[1,448,8,128]{3,1,2,0:T(8,128)(2,1)} %slice.43), channel_id=1, source_target_pairs={{0,2},{1,3},{2,4},{3,5},{4,6},{5,7},{6,8},{7,9},{8,10},{9,11},{10,... | collective-permute-start | bytes 2752520 | tf_op jit(solution)/shard_map/ppermute | solution.py:108
  25.8 132.8 %collective-permute-start.1 = (bf16[1,512,8,128]{3,1,2,0:T(8,128)(2,1)S(1)}, bf16[1,512,8,128]{3,1,2,0:T(8,128)(2,1)S(1)}, u32[]{:S(2)}, u32[]{:S(2)}) collective-permute-start(bf16[1,512,8,128]{3,1,2,0:T(8,128)(2,1)S(1)} %copy.54), channel_id=1, source_target_pairs={{0,1},{1,2},{2,3},{3,4},{4,5},{5,6},{6,7},{7,8},{8,9},{9,10},{10,1... | collective-permute-start | bytes 3145736 | tf_op jit(solution)/shard_map/ppermute | solution.py:108
  28.8 129.9 %collective-permute-start = (bf16[1,448,8,128]{3,1,2,0:T(8,128)(2,1)}, bf16[1,448,8,128]{3,1,2,0:T(8,128)(2,1)}, u32[]{:S(2)}, u32[]{:S(2)}) collective-permute-start(bf16[1,448,8,128]{3,1,2,0:T(8,128)(2,1)} %slice.42), channel_id=1, source_target_pairs={{0,2},{1,3},{2,4},{3,5},{4,6},{5,7},{6,8},{7,9},{8,10},{9,11},{10,... | collective-permute-start | bytes 2752520 | tf_op jit(solution)/shard_map/ppermute | solution.py:108
  299.4 23.4 %copy-start.10 = (pred[8,5,1024]{2,1,0:T(8,128)(4,1)}, pred[8,5,1024]{2,1,0:T(8,128)(4,1)S(1)}, u32[]{:S(2)}) copy-start(pred[8,5,1024]{2,1,0:T(8,128)(4,1)S(1)} %add_compare_fusion.2) | copy-start | bytes 122884 | tf_op jit(solution)/shard_map/while
  302.9 19.9 copy-start.3
  348.7 19.3 copy-start.22
  353.6 14.4 slice-start
  453.7 23.4 %copy-start.10 = (pred[8,5,1024]{2,1,0:T(8,128)(4,1)}, pred[8,5,1024]{2,1,0:T(8,128)(4,1)S(1)}, u32[]{:S(2)}) copy-start(pred[8,5,1024]{2,1,0:T(8,128)(4,1)S(1)} %add_compare_fusion.2) | copy-start | bytes 122884 | tf_op jit(solution)/shard_map/while
  457.2 19.9 copy-start.3
  503.0 19.3 copy-start.22
  507.9 14.4 slice-start
  598.8 18.5 copy-start.25
  598.8 18.5 copy-start.27
  598.8 18.5 copy-start.29
  620.1 23.4 %copy-start.10 = (pred[8,5,1024]{2,1,0:T(8,128)(4,1)}, pred[8,5,1024]{2,1,0:T(8,128)(4,1)S(1)}, u32[]{:S(2)}) copy-start(pred[8,5,1024]{2,1,0:T(8,128)(4,1)S(1)} %add_compare_fusion.2) | copy-start | bytes 122884 | tf_op jit(solution)/shard_map/while
  623.6 19.9 copy-start.3
  669.4 19.3 copy-start.22
  765.3 18.5 copy-start.25
  765.3 18.5 copy-start.27
  765.3 18.5 copy-start.29
  786.6 23.4 %copy-start.10 = (pred[8,5,1024]{2,1,0:T(8,128)(4,1)}, pred[8,5,1024]{2,1,0:T(8,128)(4,1)S(1)}, u32[]{:S(2)}) copy-start(pred[8,5,1024]{2,1,0:T(8,128)(4,1)S(1)} %add_compare_fusion.2) | copy-start | bytes 122884 | tf_op jit(solution)/shard_map/while
  790.0 19.9 copy-start.3
  835.8 19.3 copy-start.22
  840.7 14.4 slice-start
  931.7 18.5 copy-start.25
  931.7 18.5 copy-start.27
  931.7 18.5 copy-start.29
  953.0 23.4 %copy-start.10 = (pred[8,5,1024]{2,1,0:T(8,128)(4,1)}, pred[8,5,1024]{2,1,0:T(8,128)(4,1)S(1)}, u32[]{:S(2)}) copy-start(pred[8,5,1024]{2,1,0:T(8,128)(4,1)S(1)} %add_compare_fusion.2) | copy-start | bytes 122884 | tf_op jit(solution)/shard_map/while
  956.5 19.9 copy-start.3
  1002.2 19.3 copy-start.22
  1007.1 14.4 slice-start
  1098.0 18.5 copy-start.25
  1098.1 18.5 copy-start.27
  1098.1 18.5 copy-start.29
  1119.3 23.4 %copy-start.10 = (pred[8,5,1024]{2,1,0:T(8,128)(4,1)}, pred[8,5,1024]{2,1,0:T(8,128)(4,1)S(1)}, u32[]{:S(2)}) copy-start(pred[8,5,1024]{2,1,0:T(8,128)(4,1)S(1)} %add_compare_fusion.2) | copy-start | bytes 122884 | tf_op jit(solution)/shard_map/while
  1122.8 19.9 copy-start.3
  1168.6 19.3 copy-start.22
  1173.5 14.4 slice-start
  1264.4 18.5 copy-start.25
  1264.5 18.5 copy-start.27
  1264.5 18.5 copy-start.29
  1285.7 23.4 %copy-start.10 = (pred[8,5,1024]{2,1,0:T(8,128)(4,1)}, pred[8,5,1024]{2,1,0:T(8,128)(4,1)S(1)}, u32[]{:S(2)}) copy-start(pred[8,5,1024]{2,1,0:T(8,128)(4,1)S(1)} %add_compare_fusion.2) | copy-start | bytes 122884 | tf_op jit(solution)/shard_map/while
  1289.2 19.9 copy-start.3
  1335.0 19.3 copy-start.22
  1430.9 18.5 copy-start.25
  1430.9 18.5 copy-start.27
  1430.9 18.5 copy-start.29
  1452.2 23.4 %copy-start.10 = (pred[8,5,1024]{2,1,0:T(8,128)(4,1)}, pred[8,5,1024]{2,1,0:T(8,128)(4,1)S(1)}, u32[]{:S(2)}) copy-start(pred[8,5,1024]{2,1,0:T(8,128)(4,1)S(1)} %add_compare_fusion.2) | copy-start | bytes 122884 | tf_op jit(solution)/shard_map/while
  1455.7 19.9 copy-start.3
  1501.5 19.3 copy-start.22
  1597.4 18.5 copy-start.25
  1597.4 18.5 copy-start.27
  1597.4 18.5 copy-start.29
  1635.3 241.8 %all-to-all-start = ((bf16[1,1024,8,5,128]{4,2,3,0,1:T(8,128)(2,1)}), bf16[1,1024,8,5,128]{4,2,3,0,1:T(8,128)(2,1)}, u32[]{:S(2)}, u32[]{:S(2)}) async-start(bf16[1,1024,8,5,128]{4,2,3,0,1:T(8,128)(2,1)} %copy.72), calls=%async_computation | async-start | bytes 20971520 | tf_op jit(solution)/shard_map/all_to_all | solution.py:128
  1877.1 244.6 %all-to-all-start.1 = ((bf16[1,1024,8,5,128]{4,2,3,0,1:T(8,128)(2,1)}), bf16[1,1024,8,5,128]{4,2,3,0,1:T(8,128)(2,1)}, u32[]{:S(2)}, u32[]{:S(2)}) async-start(bf16[1,1024,8,5,128]{4,2,3,0,1:T(8,128)(2,1)} %copy.78), calls=%async_computation.1 | async-start | bytes 20971520 | tf_op jit(solution)/shard_map/all_to_all | solution.py:128
  1890.6 14.6 slice-start.7
  1898.2 242.4 %collective-permute-start.4 = (bf16[1,448,8,128]{3,2,1,0:T(8,128)(2,1)}, bf16[1,448,8,128]{3,2,1,0:T(8,128)(2,1)}, u32[]{:S(2)}, u32[]{:S(2)}) collective-permute-start(bf16[1,448,8,128]{3,2,1,0:T(8,128)(2,1)} %slice.44), channel_id=1, source_target_pairs={{2,0},{3,1},{4,2},{5,3},{6,4},{7,5},{8,6},{9,7},{10,8},{11,9},{12,... | collective-permute-start | bytes 2752520 | tf_op jit(solution)/shard_map/ppermute | solution.py:122
  1899.5 262.3 %collective-permute-start.5 = (bf16[1,512,8,128]{3,2,1,0:T(8,128)(2,1)}, bf16[1,512,8,128]{3,2,1,0:T(8,128)(2,1)}, u32[]{:S(2)}, u32[]{:S(2)}) collective-permute-start(bf16[1,512,8,128]{3,2,1,0:T(8,128)(2,1)} %slice.45), channel_id=1, source_target_pairs={{1,0},{2,1},{3,2},{4,3},{5,4},{6,5},{7,6},{8,7},{9,8},{10,9},{11,1... | collective-permute-start | bytes 3145736 | tf_op jit(solution)/shard_map/ppermute | solution.py:122
  1901.8 263.6 %collective-permute-start.6 = (bf16[1,448,8,128]{3,2,1,0:T(8,128)(2,1)}, bf16[1,448,8,128]{3,2,1,0:T(8,128)(2,1)}, u32[]{:S(2)}, u32[]{:S(2)}) collective-permute-start(bf16[1,448,8,128]{3,2,1,0:T(8,128)(2,1)} %slice.46), channel_id=1, source_target_pairs={{2,0},{3,1},{4,2},{5,3},{6,4},{7,5},{8,6},{9,7},{10,8},{11,9},{12,... | collective-permute-start | bytes 2752520 | tf_op jit(solution)/shard_map/ppermute | solution.py:122
  1903.1 279.8 %collective-permute-start.7 = (bf16[1,512,8,128]{3,2,1,0:T(8,128)(2,1)}, bf16[1,512,8,128]{3,2,1,0:T(8,128)(2,1)S(1)}, u32[]{:S(2)}, u32[]{:S(2)}) collective-permute-start(bf16[1,512,8,128]{3,2,1,0:T(8,128)(2,1)} %slice.47), channel_id=1, source_target_pairs={{1,0},{2,1},{3,2},{4,3},{5,4},{6,5},{7,6},{8,7},{9,8},{10,9},{11,1... | collective-permute-start | bytes 3145736 | tf_op jit(solution)/shard_map/ppermute | solution.py:122
  (220 other events, 1465.0 us)
Sparse Core Ops, SparseCore 0:
  11.1 149.4 all-gather.6
  162.8 97.3 all-gather.4
where the time goes:
time: 2200 us; the launch traced here: 2190 us
  matrix products  853 us (39%)
  waiting for transfers between devices  681 us (31%)
  local copies, waits for them, and re-layouts  482 us (22%)
  other arithmetic  96.8 us (4%)
  starting transfers between devices  34.9 us (2%)
  loops' own time  31.9 us (1%)
    all_to_all x2, waiting for transfers between devices, owner_sum(): lax.all_to_all(contrib.astype(jnp.bfloat16), 'cp', 1, 1, tiled=True)  421 us
    dot_general x8, matrix products, body(): jnp.einsum('bguij,bigud->bjgud', ds_str, q_blk, preferred_element_type=jn...  141 us
    dot_general x8, matrix products, body(): jnp.einsum('bguij,bigud->bjgud', pb_str, do_blk, preferred_element_type=j...  141 us
    ppermute x4, waiting for transfers between devices, fetch_halo(): lax.ppermute(tail_part, 'cp', [(sender, sender + dist) for sender in rang...  123 us
    dot_general x8, matrix products, body(): jnp.einsum('bigud,bjgud->bguij', do_blk, v_str, preferred_element_type=jn...  117 us
    dynamic_update_slice x16, local copies, waits for them, and re-layouts, body(): lax.dynamic_update_slice_in_dim(dv_ext, lax.dynamic_slice_in_dim(dv_ext,...  102 us
    dot_general x8, matrix products, body(): jnp.einsum('bigud,bjgud->bguij', q_blk, k_str, preferred_element_type=jnp...  98.6 us
    all_gather x1, waiting for transfers between devices, per_device(): lax.all_gather(compact(k_rope, group_size), 'cp', axis=1, tiled=True)  86.2 us
  transfers between devices with their start and end apart: 12, of which 8 were waited for; matrix products, arithmetic and copies ran while one was open for 4% of the time, Pallas kernels for 0%

commit v1 on v0

v1 whole, which is shorter than its diff:
```python
import functools

import jax
import jax.numpy as jnp
from jax import lax
from jax.experimental import pallas as pl
from jax.experimental.pallas import tpu as pltpu
from jax.sharding import PartitionSpec as P

BLOCK = 64
LOCAL = 16
STRIDE = 8
HALO = (LOCAL - 1) * BLOCK
ROWS = 256
CHUNK = 128
LOG2E = 1.4426950408889634
CHUNKS = 2
F32 = jnp.float32
BF16 = jnp.bfloat16


def residue(kv_head, member, group_size):
    return (-1 - (kv_head * group_size + member)) % STRIDE


def fold(x, op):
    rows, cols = x.shape
    return op(x.reshape(rows // 8, 8, cols), axis=0)


def pieces(total):
    return [(start, min(CHUNK, total - start)) for start in range(0, total, CHUNK)]


def attention_kernel(first_head, group_size, q_ref, do_ref, k_ref, v_ref, ks_ref, vs_ref,
                     o_ref, dq_ref, dk_own_ref, dv_own_ref, dk_halo_ref, dv_halo_ref, dks_ref, dvs_ref,
                     k_t, v_t, ks_t, vs_t, dk_acc, dv_acc, e_loc, e_str, pb_loc, pb_str, ds_loc, ds_str):
    shard = lax.axis_index('cp')
    head_idx, member = pl.program_id(0), pl.program_id(1)
    seq_loc, head_dim = q_ref.shape[2], q_ref.shape[3]
    n_tiles = seq_loc // ROWS
    win = HALO + ROWS
    win_pad = pb_loc.shape[1]
    n_str = ks_t.shape[1]
    scale = 1.0 / head_dim
    to_exp2 = scale * LOG2E
    jres = lax.rem(STRIDE * 64 - 1 - ((first_head + head_idx) * group_size + member), STRIDE)
    neg = -jnp.inf

    @pl.when((head_idx == 0) & (member == 0))
    def _():
        for t in range(n_tiles):
            pb_loc[t, win:, :] = jnp.zeros((win_pad - win, ROWS), BF16)
            ds_loc[t, win:, :] = jnp.zeros((win_pad - win, ROWS), BF16)

    @pl.when(member == 0)
    def _():
        k_t[...] = k_ref[0, 0].T
        v_t[...] = v_ref[0, 0].T
        dk_acc[...] = jnp.zeros_like(dk_acc)
        dv_acc[...] = jnp.zeros_like(dv_acc)

    def str_rows(ref, start, size):
        return ref[start // BLOCK:(start + size) // BLOCK, 0, 0, 0].reshape(size, head_dim)

    ks_t[...] = str_rows(ks_ref, 0, n_str).T
    vs_t[...] = str_rows(vs_ref, 0, n_str).T

    y_row = lax.broadcasted_iota(jnp.int32, (1, ROWS), 1)
    st = [dict() for _ in range(n_tiles)]
    for t in range(n_tiles):
        st[t]['q_t'] = q_ref[0, 0, t * ROWS:(t + 1) * ROWS, :].T
        st[t]['do_t'] = do_ref[0, 0, t * ROWS:(t + 1) * ROWS, :].T
        st[t]['thr'] = shard - 1 - ((y_row // BLOCK + t * (ROWS // BLOCK)) < jres).astype(jnp.int32)

    def score_steps(t):
        s = st[t]

        def local(start, size):
            def run():
                sc = jnp.dot(k_ref[0, 0, t * ROWS + start:t * ROWS + start + size, :], s['q_t'], preferred_element_type=F32)
                for off in range(0, size, BLOCK):
                    x0 = start + off
                    sub = sc[off:off + BLOCK]
                    if x0 < HALO:
                        seen = t * ROWS + x0 >= HALO - seq_loc * shard
                        sub = sub + jnp.where(seen, 0.0, neg).astype(F32)
                    if x0 < ROWS - BLOCK:
                        sub = jnp.where(y_row < x0 + BLOCK, sub, neg)
                    if x0 >= HALO:
                        col = lax.broadcasted_iota(jnp.int32, (BLOCK, ROWS), 0)
                        row = lax.broadcasted_iota(jnp.int32, (BLOCK, ROWS), 1)
                        sub = jnp.where(col + (x0 - HALO) <= row, sub, neg)
                    e_loc[t, x0:x0 + BLOCK, :] = sub
                    part = fold(sub, jnp.max)
                    s['mx'] = part if 'mx' not in s else jnp.maximum(s['mx'], part)
            return run

        def strided(start, size):
            def run():
                sc = jnp.dot(str_rows(ks_ref, start, size), s['q_t'], preferred_element_type=F32)
                for off in range(0, size, BLOCK):
                    x0 = start + off
                    sub = sc[off:off + BLOCK] + jnp.where(x0 // BLOCK < s['thr'], 0.0, neg).astype(F32)
                    e_str[t, x0:x0 + BLOCK, :] = sub
                    s['mx'] = jnp.maximum(s['mx'], fold(sub, jnp.max))
            return run

        def finish():
            s['m'] = jnp.max(s['mx'], axis=0, keepdims=True)
        return [local(*p) for p in pieces(win)] + [strided(*p) for p in pieces(n_str)] + [finish]

    def exp_steps(t):
        s = st[t]

        def one(ref, start, size):
            def run():
                e = jnp.exp2((ref[t, start:start + size, :] - s['m']) * to_exp2)
                ref[t, start:start + size, :] = e
                part = fold(e, jnp.sum)
                s['l'] = part if 'l' not in s else s['l'] + part
            return run

        def finish():
            s['inv'] = 1.0 / jnp.sum(s['l'], axis=0, keepdims=True)
        return [one(e_loc, *p) for p in pieces(win)] + [one(e_str, *p) for p in pieces(n_str)] + [finish]

    def out_steps(t):
        s = st[t]

        def loc(start, size):
            def run():
                pb_loc[t, start:start + size, :] = (e_loc[t, start:start + size, :] * s['inv']).astype(BF16)
            return run

        def strided(start, size):
            def run():
                pb_str[start:start + size, t * ROWS:(t + 1) * ROWS] = (e_str[t, start:start + size, :] * s['inv']).astype(BF16)
            return run

        def finish():
            o_t = (jnp.dot(v_t[:, t * ROWS:t * ROWS + win_pad], pb_loc[t], preferred_element_type=F32)
                   + jnp.dot(vs_t[...], pb_str[:, t * ROWS:(t + 1) * ROWS], preferred_element_type=F32))
            s['delta'] = jnp.sum(s['do_t'].astype(F32) * o_t, axis=0, keepdims=True)
            o_ref[0, 0, t * ROWS:(t + 1) * ROWS, :] = o_t.T.astype(BF16)
        return [loc(*p) for p in pieces(win)] + [strided(*p) for p in pieces(n_str)] + [finish]

    def grad_steps(t):
        s = st[t]

        def loc(start, size):
            def run():
                dp = jnp.dot(v_ref[0, 0, t * ROWS + start:t * ROWS + start + size, :], s['do_t'], preferred_element_type=F32)
                p = e_loc[t, start:start + size, :] * s['inv']
                ds_loc[t, start:start + size, :] = (p * (dp - s['delta'])).astype(BF16)
            return run

        def strided(start, size):
            def run():
                dp = jnp.dot(str_rows(vs_ref, start, size), s['do_t'], preferred_element_type=F32)
                p = e_str[t, start:start + size, :] * s['inv']
                ds_str[start:start + size, t * ROWS:(t + 1) * ROWS] = (p * (dp - s['delta'])).astype(BF16)
            return run
        return [loc(*p) for p in pieces(win)] + [strided(*p) for p in pieces(n_str)]

    def back_steps(t):
        def dv():
            dv_acc[t * ROWS:t * ROWS + win, :] += jnp.dot(pb_loc[t, :win, :], do_ref[0, 0, t * ROWS:(t + 1) * ROWS, :], preferred_element_type=F32)

        def dk():
            dk_acc[t * ROWS:t * ROWS + win, :] += jnp.dot(ds_loc[t, :win, :], q_ref[0, 0, t * ROWS:(t + 1) * ROWS, :], preferred_element_type=F32)

        def dq():
            dq_t = (jnp.dot(k_t[:, t * ROWS:t * ROWS + win_pad], ds_loc[t], preferred_element_type=F32)
                    + jnp.dot(ks_t[...], ds_str[:, t * ROWS:(t + 1) * ROWS], preferred_element_type=F32))
            dq_ref[0, 0, t * ROWS:(t + 1) * ROWS, :] = (dq_t * scale).T.astype(BF16)
        return [dv, dk, dq]

    def weave(*lists):
        total = max(len(x) for x in lists)
        for i in range(total):
            for x in lists:
                for j in range(i * len(x) // total, (i + 1) * len(x) // total):
                    x[j]()

    weave(score_steps(0))
    for t in range(n_tiles):
        later = score_steps(t + 1) if t + 1 < n_tiles else []
        earlier = back_steps(t - 1) if t > 0 else []
        weave(*[x for x in (exp_steps(t), later, earlier) if x])
        weave(out_steps(t))
        weave(grad_steps(t))
    weave(back_steps(n_tiles - 1))

    n_blk = n_str // BLOCK
    dvs = jnp.dot(pb_str[...], do_ref[0, 0], preferred_element_type=F32)
    dvs_ref[:n_blk, 0, 0] = dvs.reshape(n_blk, BLOCK, head_dim)
    dks = jnp.dot(ds_str[...], q_ref[0, 0], preferred_element_type=F32) * scale
    dks_ref[:n_blk, 0, 0] = dks.reshape(n_blk, BLOCK, head_dim)
    rest = dks_ref.shape[0] - n_blk
    dks_ref[n_blk:, 0, 0] = jnp.zeros((rest, BLOCK, head_dim), F32)
    dvs_ref[n_blk:, 0, 0] = jnp.zeros((rest, BLOCK, head_dim), F32)

    @pl.when(member == group_size - 1)
    def _():
        dk_own_ref[0] = dk_acc[HALO:HALO + seq_loc, :] * scale
        dv_own_ref[0] = dv_acc[HALO:HALO + seq_loc, :]
        dk_halo_ref[0] = (dk_acc[:HALO, :] * scale).astype(BF16)
        dv_halo_ref[0] = dv_acc[:HALO, :].astype(BF16)


def attention(first_head, n_heads, q, d_out, kv_ext, kv_str):
    _, group_size, seq_loc, head_dim = q.shape
    ext_pad = kv_ext.shape[2]
    cp_size = kv_str.shape[0]
    n_blk = cp_size - 2
    n_str = n_blk * BLOCK
    win = HALO + ROWS
    win_pad = -(-win // 256) * 256
    n_tiles = seq_loc // ROWS
    spec_q = pl.BlockSpec((1, 1, seq_loc, head_dim), lambda g, u: (first_head + g, u, 0, 0))
    spec_o = pl.BlockSpec((1, 1, seq_loc, head_dim), lambda g, u: (g, u, 0, 0))
    ext = [pl.BlockSpec((1, 1, ext_pad, head_dim), lambda g, u, w=w: (w, first_head + g, 0, 0)) for w in range(2)]
    strided = [pl.BlockSpec((n_blk, 1, 1, 1, BLOCK, head_dim), lambda g, u, w=w: (0, w, g, u, 0, 0)) for w in range(2)]
    spec_own = pl.BlockSpec((1, seq_loc, head_dim), lambda g, u: (g, 0, 0))
    spec_halo = pl.BlockSpec((1, HALO, head_dim), lambda g, u: (g, 0, 0))
    spec_str = pl.BlockSpec((cp_size, 1, 1, BLOCK, head_dim), lambda g, u: (0, g, u, 0, 0))
    sds = jax.ShapeDtypeStruct
    flops = n_heads * group_size * 6 * 2 * seq_loc * (win + n_str) * head_dim
    return pl.pallas_call(
        functools.partial(attention_kernel, first_head, group_size),
        grid=(n_heads, group_size),
        in_specs=[spec_q, spec_q, ext[0], ext[1], strided[0], strided[1]],
        out_specs=[spec_o, spec_o, spec_own, spec_own, spec_halo, spec_halo, spec_str, spec_str],
        out_shape=[
            sds((n_heads, group_size, seq_loc, head_dim), BF16), sds((n_heads, group_size, seq_loc, head_dim), BF16),
            sds((n_heads, seq_loc, head_dim), F32), sds((n_heads, seq_loc, head_dim), F32),
            sds((n_heads, HALO, head_dim), BF16), sds((n_heads, HALO, head_dim), BF16),
            sds((cp_size, n_heads, group_size, BLOCK, head_dim), F32), sds((cp_size, n_heads, group_size, BLOCK, head_dim), F32),
        ],
        scratch_shapes=[
            pltpu.VMEM((head_dim, ext_pad), BF16), pltpu.VMEM((head_dim, ext_pad), BF16),
            pltpu.VMEM((head_dim, n_str), BF16), pltpu.VMEM((head_dim, n_str), BF16),
            pltpu.VMEM((HALO + seq_loc, head_dim), F32), pltpu.VMEM((HALO + seq_loc, head_dim), F32),
            pltpu.VMEM((n_tiles, win, ROWS), F32), pltpu.VMEM((n_tiles, n_str, ROWS), F32),
            pltpu.VMEM((n_tiles, win_pad, ROWS), BF16), pltpu.VMEM((n_str, seq_loc), BF16),
            pltpu.VMEM((n_tiles, win_pad, ROWS), BF16), pltpu.VMEM((n_str, seq_loc), BF16),
        ],
        compiler_params=pltpu.CompilerParams(vmem_limit_bytes=48 * 1024 * 1024),
        cost_estimate=pl.CostEstimate(flops=flops, bytes_accessed=0, transcendentals=0),
        name='attention',
    )(q, d_out, kv_ext, kv_ext, kv_str, kv_str)


def halo_lengths(seq_loc):
    hop_count = -(-HALO // seq_loc)
    return [seq_loc] * (hop_count - 1) + [HALO - (hop_count - 1) * seq_loc]


def solution(mesh):
    cp_size = mesh.shape['cp']
    spec = P('dp', 'cp', None, None)

    def per_device(q_rope, k_rope, values, d_out):
        seq_loc, heads, head_dim = q_rope.shape[1:]
        kv_heads = k_rope.shape[2]
        group_size = heads // kv_heads
        lengths = halo_lengths(seq_loc)
        n_res = seq_loc // BLOCK
        kv = jnp.stack([jnp.swapaxes(k_rope[0], 0, 1), jnp.swapaxes(values[0], 0, 1)])
        kvb = kv.reshape(2, kv_heads, n_res, BLOCK, head_dim)
        kv_c = jnp.stack([jnp.stack([kvb[:, g, residue(g, u, group_size)] for u in range(group_size)], 1) for g in range(kv_heads)], 1)
        parts = []
        for dist in range(len(lengths), 0, -1):
            tail = kv[:, :, seq_loc - lengths[dist - 1]:]
            parts.append(lax.ppermute(tail, 'cp', [(s, s + dist) for s in range(cp_size - dist)]))
        per = kv_heads // CHUNKS
        gathered = [lax.all_gather(kv_c[:, i * per:(i + 1) * per], 'cp', axis=0, tiled=False) for i in range(CHUNKS)]
        pad = -(HALO + seq_loc) % 256
        kv_ext = jnp.concatenate(parts + [kv, jnp.zeros((2, kv_heads, pad, head_dim), BF16)], axis=2)

        def head_major(x):
            return jnp.transpose(x[0].reshape(seq_loc, kv_heads, group_size, head_dim), (1, 2, 0, 3))

        q_h, do_h = head_major(q_rope), head_major(d_out)
        outs = [attention(i * per, per, q_h, do_h, kv_ext, gathered[i]) for i in range(CHUNKS)]
        strided = [[lax.psum_scatter(out[6 + w], 'cp', scatter_dimension=0, tiled=False) for out in outs] for w in range(2)]

        def token_major(xs):
            x = jnp.concatenate(xs, axis=0)
            return jnp.transpose(x, (2, 0, 1, 3)).reshape(1, seq_loc, heads, head_dim)

        attn_out = token_major([out[0] for out in outs])
        d_q = token_major([out[1] for out in outs])

        def finish(w):
            own = jnp.concatenate([out[2 + w] for out in outs], axis=0)
            halo = jnp.concatenate([out[4 + w] for out in outs], axis=0)
            offset = 0
            total = own
            for dist in range(len(lengths), 0, -1):
                size = lengths[dist - 1]
                arrived = lax.ppermute(halo[:, offset:offset + size], 'cp', [(s + dist, s) for s in range(cp_size - dist)])
                offset += size
                total = total + jnp.pad(arrived, ((0, 0), (seq_loc - size, 0), (0, 0))).astype(F32)
            got = jnp.concatenate(strided[w], axis=0)
            zero = jnp.zeros((BLOCK, head_dim), F32)
            rows = []
            for g in range(kv_heads):
                by_res = {residue(g, u, group_size): u for u in range(group_size)}
                rows.append(jnp.concatenate([got[g, by_res[r]] if r in by_res else zero for r in range(n_res)], axis=0))
            total = total + jnp.stack(rows)
            return jnp.swapaxes(total.astype(BF16), 0, 1)[None]

        return attn_out, d_q, finish(0), finish(1)

    return jax.shard_map(per_device, mesh=mesh, in_specs=(spec, spec, spec, spec), out_specs=(spec, spec, spec, spec), check_vma=False)
```

time: 2200 us -> 641 us (0.29)
  matrix products: 853 us -> 0 us
  local copies, waits for them, and re-layouts: 482 us -> 101 us
  waiting for transfers between devices: 681 us -> 310 us
  Pallas kernels: 0 us -> 181 us
  other arithmetic: 96.8 us -> 13.8 us
  loops' own time: 31.9 us -> 0 us
    dot_general x100 -> x0, matrix products: 853 us -> none  [the longest x8 141 us: body(): jnp.einsum('bguij,bigud->bjgud', ds_str, q_blk, preferred_element_type=jn...]
    all_to_all x2 -> x0, waiting for transfers between devices: 421 us -> none  [owner_sum(): lax.all_to_all(contrib.astype(jnp.bfloat16), 'cp', 1, 1, tiled=True)]
    reduce_scatter x0 -> x4, waiting for transfers between devices: none -> 211 us  [per_device(): lax.psum_scatter(out[6 + w], 'cp', scatter_dimension=0, tiled=False)]
    dynamic_slice x72 -> x0, local copies, waits for them, and re-layouts: 192 us -> none  [the longest x16 80.7 us: body(): lax.dynamic_slice_in_dim(dk_ext, win_start, window, axis=1) + dk_win]
    pallas_call x0 -> x2, Pallas kernels: none -> 181 us  [attention(): pl.pallas_call(functools.partial(attention_kernel, first_head, group_size...]
    dynamic_update_slice x32 -> x0, local copies, waits for them, and re-layouts: 153 us -> none  [the longest x16 102 us: body(): lax.dynamic_update_slice_in_dim(dv_ext, lax.dynamic_slice_in_dim(dv_ext,...]
    all_gather x2, waiting for transfers between devices: 86.2 us -> 0.01 us  [per_device(): lax.all_gather(kv_c[:, i * per:(i + 1) * per], 'cp', axis=0, tiled=False)]
    while x530 -> x0, local copies, waits for them, and re-layouts: 85.5 us -> none
  transfers between devices with their start and end apart: 12 -> 12, of which waited for: 8 -> 4; matrix products, arithmetic and copies ran while one was open for 4% -> 16% of each run, Pallas kernels for 0% -> 28%
where the time goes in v1:
time: 641 us; the launch traced here: 637 us
  waiting for transfers between devices  310 us (48%)
  Pallas kernels  181 us (28%)
  local copies, waits for them, and re-layouts  101 us (16%)
  starting transfers between devices  16.5 us (3%)
  between operations  14.6 us (2%)
  other arithmetic  13.8 us (2%)
    reduce_scatter x4, waiting for transfers between devices, per_device(): lax.psum_scatter(out[6 + w], 'cp', scatter_dimension=0, tiled=False)  211 us
    pallas_call x2, Pallas kernels, attention(): pl.pallas_call(functools.partial(attention_kernel, first_head, group_size...  181 us
    ppermute x2, waiting for transfers between devices, per_device(): lax.ppermute(tail, 'cp', [(s, s + dist) for s in range(cp_size - dist)])  97 us
    unnamed x99, local copies, waits for them, and re-layouts  77.6 us
  transfers between devices with their start and end apart: 12, of which 4 were waited for; matrix products, arithmetic and copies ran while one was open for 16% of the time, Pallas kernels for 28%

profile of v1, /device:TPU:21, one launch (start us, length us, event | category | flops | bytes accessed | tf_op | source)
XLA Modules:
  0.0 637.1 jit_solution(7293288976718244959)
XLA Ops:
  7.2 3.4 fusion.10
  11.6 0.9 pad_maximum_fusion.3
  14.8 5.1 collective-permute-start.1
  20.1 4.3 collective-permute-start
  24.5 6.1 copy.26
  30.6 3.6 copy.27
  34.3 97.0 %collective-permute-done = bf16[2,8,448,128]{3,2,1,0:T(8,128)(2,1)S(1)} collective-permute-done((bf16[2,8,448,128]{3,2,1,0:T(8,128)(2,1)S(1)}, bf16[2,8,448,128]{3,2,1,0:T(8,128)(2,1)S(1)}, u32[]{:S(2)}, u32[]{:S(2)}) %collective-permute-start) | collective-permute-done | bytes 1835040 | tf_op jit(solution)/shard_map/ppermute | solution.py:276
  131.3 6.7 %maximum_maximum_fusion.k_ref.v_ref = bf16[2,8,1536,128]{3,2,1,0:T(8,128)(2,1)} fusion(bf16[1,8,512,128]{3,2,1,0:T(8,128)(2,1)S(1)} %copy-done.9, bf16[1,8,512,128]{3,2,1,0:T(8,128)(2,1)S(1)} %get-tuple-element.76, bf16[2,8,512,128]{3,2,1,0:T(8,128)(2,1)S(1)} %collective-permute-done.1, bf16[2,8,448,128]{3,2,1,0:T(8,128)(2,1)S(1)} %collective-permute-done, ...), kind=kLoop, calls=%fused_computation | loop fusion | flops 31457280 | bytes 12323840 | tf_op jit(solution)/shard_map/concatenate | solution.py:280
  138.1 11.7 %copy.32 = bf16[32,4,5,64,128]{4,3,2,1,0:T(8,128)(2,1)} copy(bf16[32,4,5,64,128]{4,3,0,2,1:T(8,128)(2,1)} %all-gather.5.cloned.1.call-done) | data formatting | bytes 20971520 | tf_op jit(solution)/shard_map/all_gather | solution.py:278
  149.8 90.6 %attention.2 = (bf16[4,5,512,128]{3,2,1,0:T(8,128)(2,1)}, bf16[4,5,512,128]{3,2,1,0:T(8,128)(2,1)}, f32[4,512,128]{2,1,0:T(8,128)S(1)}, f32[4,512,128]{2,1,0:T(8...) custom-call(bf16[8,5,512,128]{3,2,1,0:T(8,128)(2,1)} %bitcast.617, ...), custom_call_target="tpu_custom_call" | custom-call | flops 33218887680 | tf_op jit(solution)/shard_map/attention/pallas_call | solution.py:230
  240.4 0.9 copy-done.4
  241.4 0.9 copy-done.2
  242.3 90.7 %attention.3 = (bf16[4,5,512,128]{3,2,1,0:T(8,128)(2,1)}, bf16[4,5,512,128]{3,2,1,0:T(8,128)(2,1)}, f32[4,512,128]{2,1,0:T(8,128)S(1)}, f32[4,512,128]{2,1,0:T(8...) custom-call(bf16[8,5,512,128]{3,2,1,0:T(8,128)(2,1)} %bitcast.618, ...), custom_call_target="tpu_custom_call" | custom-call | flops 33218887680 | tf_op jit(solution)/shard_map/attention/pallas_call | solution.py:230
  333.0 1.0 copy-done
  333.9 0.9 copy-done.5
  334.9 0.9 copy-done.7
  340.3 1.3 constant_dynamic-update-slice_fusion.41
  341.7 1.0 slice.506
  342.8 1.0 slice.507
  344.6 1.0 slice.548
  345.5 1.1 slice.549
  346.6 1.1 copy-done.11
  348.2 5.7 copy.40
  353.9 1.3 collective-permute-start.2
  355.2 2.0 collective-permute-start.3
  357.2 1.3 collective-permute-start.4
  358.5 2.2 collective-permute-start.5
  361.2 5.7 copy.41
  366.9 1.5 constant_dynamic-update-slice_fusion.126
  369.1 1.5 constant_dynamic-update-slice_fusion.124
  370.5 1.5 constant_dynamic-update-slice_fusion.123
  372.6 1.5 constant_dynamic-update-slice_fusion.122
  374.1 1.5 constant_dynamic-update-slice_fusion.121
  376.2 84.1 %reduce-scatter.11.cloned.1.call-done = f32[1,4,5,64,128]{4,3,2,1,0:T(8,128)} async-done(((f32[16,4,5,64,128]{4,3,2,1,0:T(8,128)}), f32[1,4,5,64,128]{4,3,2,1,0:T(8,128)}) %reduce-scatter.11.cloned.1.call-update) | async-done | bytes 655376 | tf_op jit(solution)/shard_map/reduce_scatter | solution.py:287
  460.3 1.5 constant_dynamic-update-slice_fusion.151
  461.8 1.5 constant_dynamic-update-slice_fusion.150
  463.9 1.5 constant_dynamic-update-slice_fusion.149
  465.4 1.5 constant_dynamic-update-slice_fusion.148
  467.5 1.5 constant_dynamic-update-slice_fusion.147
  469.6 63.6 %reduce-scatter.7.cloned.1.call-done = f32[1,4,5,64,128]{4,3,2,1,0:T(8,128)} async-done(((f32[16,4,5,64,128]{4,3,2,1,0:T(8,128)}), f32[1,4,5,64,128]{4,3,2,1,0:T(8,128)}) %reduce-scatter.7.cloned.1.call-update) | async-done | bytes 655376 | tf_op jit(solution)/shard_map/reduce_scatter | solution.py:287
  533.1 1.5 constant_dynamic-update-slice_fusion.91
  534.6 1.5 constant_dynamic-update-slice_fusion.90
  536.8 1.5 constant_dynamic-update-slice_fusion.89
  538.2 1.5 constant_dynamic-update-slice_fusion.88
  540.4 1.5 constant_dynamic-update-slice_fusion.87
  542.5 63.6 %reduce-scatter.5.cloned.1.call-done = f32[1,4,5,64,128]{4,3,2,1,0:T(8,128)} async-done(((f32[16,4,5,64,128]{4,3,2,1,0:T(8,128)}), f32[1,4,5,64,128]{4,3,2,1,0:T(8,128)}) %reduce-scatter.5.cloned.1.call-update) | async-done | bytes 655376 | tf_op jit(solution)/shard_map/reduce_scatter | solution.py:287
  606.1 1.5 constant_dynamic-update-slice_fusion.66
  607.6 1.4 constant_dynamic-update-slice_fusion.64
  609.1 1.4 constant_dynamic-update-slice_fusion.63
  610.5 1.4 constant_dynamic-update-slice_fusion.62
  611.9 1.4 constant_dynamic-update-slice_fusion.61
  614.0 1.0 constant_dynamic-update-slice_fusion.97
  615.1 1.0 constant_dynamic-update-slice_fusion.95
  616.1 1.0 constant_dynamic-update-slice_fusion.93
  617.1 1.0 constant_dynamic-update-slice_fusion.92
  618.1 1.9 fusion.8
  620.0 1.6 copy.42
  621.7 1.0 constant_dynamic-update-slice_fusion.158
  622.7 1.0 constant_dynamic-update-slice_fusion.156
  623.7 1.0 constant_dynamic-update-slice_fusion.155
  624.7 1.0 constant_dynamic-update-slice_fusion.153
  625.7 1.0 constant_dynamic-update-slice_fusion.152
  626.7 1.9 fusion.7
  628.6 1.6 copy.43
  (110 shorter events, 16.3 us)
Async XLA Ops:
  7.2 130.9 %all-gather.5.cloned.1.call-start = ((), (), s32[]{:S(2)}) async-start(), calls=%async_computation.8 | async-start | bytes 11141120 | tf_op jit(solution)/shard_map/all_gather | solution.py:278
  10.9 0.7 copy-start.18
  12.6 229.7 %all-gather.7.cloned.1.call-start = ((), (), s32[]{:S(2)}) async-start(), calls=%async_computation.9 | async-start | bytes 11141120 | tf_op jit(solution)/shard_map/all_gather | solution.py:278
  12.7 0.9 copy-start.19
  12.7 1.9 copy-start.9
  14.5 352.4 %reduce-scatter.9.cloned.1.call-start = ((), (), s32[]{:S(2)}) async-start(), calls=%async_computation.6 | async-start | bytes 11141120 | tf_op jit(solution)/shard_map/reduce_scatter | solution.py:287
  14.8 116.5 %collective-permute-start.1 = (bf16[2,8,512,128]{3,2,1,0:T(8,128)(2,1)S(1)}, bf16[2,8,512,128]{3,2,1,0:T(8,128)(2,1)S(1)}, u32[]{:S(2)}, u32[]{:S(2)}) collective-permute-start(bf16[2,8,512,128]{3,2,1,0:T(8,128)(2,1)S(1)} %pad_maximum_fusion.2), channel_id=1, source_target_pairs={{0,1},{1,2},{2,3},{3,4},{4,5},{5,6},{6,7},{7,8},{8,9},{9,10},{10,1... | collective-permute-start | bytes 6291464 | tf_op jit(solution)/shard_map/ppermute | solution.py:276
  19.9 10.7 %slice-start = ((s8[5242880]{0:T(1024)(128)(4,1)}), s8[4194304]{0:T(1024)(128)(4,1)S(1)}, s32[]{:S(2)}) async-start(s8[5242880]{0:T(1024)(128)(4,1)} %bitcast.615), calls=%async_computation.10 | async-start | bytes 8388608
  20.1 10.5 %slice-start.1 = ((s8[5242880]{0:T(1024)(128)(4,1)}), s8[1048576]{0:T(1024)(128)(4,1)S(1)}, s32[]{:S(2)}) async-start(s8[5242880]{0:T(1024)(128)(4,1)} %bitcast.615), calls=%async_computation.11 | async-start | bytes 2097152
  20.1 111.2 %collective-permute-start = (bf16[2,8,448,128]{3,2,1,0:T(8,128)(2,1)S(1)}, bf16[2,8,448,128]{3,2,1,0:T(8,128)(2,1)S(1)}, u32[]{:S(2)}, u32[]{:S(2)}) collective-permute-start(bf16[2,8,448,128]{3,2,1,0:T(8,128)(2,1)S(1)} %fusion.6), channel_id=1, source_target_pairs={{0,2},{1,3},{2,4},{3,5},{4,6},{5,7},{6,8},{7,9},{8,10},{9,11},{10,... | collective-permute-start | bytes 5505032 | tf_op jit(solution)/shard_map/ppermute | solution.py:276
  240.4 0.9 copy-start.4
  241.3 1.0 copy-start.2
  242.3 218.0 %reduce-scatter.11.cloned.1.call-start = ((), (), s32[]{:S(2)}) async-start(), calls=%async_computation.7 | async-start | bytes 11141120 | tf_op jit(solution)/shard_map/reduce_scatter | solution.py:287
  333.0 1.0 copy-start
  333.9 0.9 copy-start.5
  334.9 0.9 copy-start.7
  335.9 197.3 %reduce-scatter.7.cloned.1.call-start = ((), (), s32[]{:S(2)}) async-start(), calls=%async_computation.5 | async-start | bytes 11141120 | tf_op jit(solution)/shard_map/reduce_scatter | solution.py:287
  336.5 269.6 %reduce-scatter.5.cloned.1.call-start = ((), (), s32[]{:S(2)}) async-start(), calls=%async_computation.4 | async-start | bytes 11141120 | tf_op jit(solution)/shard_map/reduce_scatter | solution.py:287
  337.2 4.4 copy-start.8
  341.7 2.1 copy-start.3
  342.8 1.7 copy-start.6
  344.4 2.2 copy-start.13
  344.6 3.1 copy-start.11
  348.2 12.6 %copy-start.10 = (bf16[4,5,512,128]{3,2,1,0:T(8,128)(2,1)S(1)}, bf16[4,5,512,128]{3,2,1,0:T(8,128)(2,1)}, u32[]{:S(2)}) copy-start(bf16[4,5,512,128]{3,2,1,0:T(8,128)(2,1)} %get-tuple-element.22) | copy-start | bytes 7864324
  348.2 12.6 %copy-start.12 = (bf16[4,5,512,128]{3,2,1,0:T(8,128)(2,1)S(1)}, bf16[4,5,512,128]{3,2,1,0:T(8,128)(2,1)}, u32[]{:S(2)}) copy-start(bf16[4,5,512,128]{3,2,1,0:T(8,128)(2,1)} %get-tuple-element.23) | copy-start | bytes 7864324
  353.9 264.2 %collective-permute-start.2 = (bf16[8,448,128]{2,1,0:T(8,128)(2,1)}, bf16[8,448,128]{2,1,0:T(8,128)(2,1)}, u32[]{:S(2)}, u32[]{:S(2)}) collective-permute-start(bf16[8,448,128]{2,1,0:T(8,128)(2,1)} %slice.506), channel_id=1, source_target_pairs={{2,0},{3,1},{4,2},{5,3},{6,4},{7,5},{8,6},{9,7},{10,8},{11,9},{12,... | collective-permute-start | bytes 2752520 | tf_op jit(solution)/shard_map/ppermute | solution.py:303
  355.2 262.9 %collective-permute-start.3 = (bf16[8,512,128]{2,1,0:T(8,128)(2,1)}, bf16[8,512,128]{2,1,0:T(8,128)(2,1)}, u32[]{:S(2)}, u32[]{:S(2)}) collective-permute-start(bf16[8,512,128]{2,1,0:T(8,128)(2,1)} %slice.507), channel_id=1, source_target_pairs={{1,0},{2,1},{3,2},{4,3},{5,4},{6,5},{7,6},{8,7},{9,8},{10,9},{11,1... | collective-permute-start | bytes 3145736 | tf_op jit(solution)/shard_map/ppermute | solution.py:303
  357.2 269.5 %collective-permute-start.4 = (bf16[8,448,128]{2,1,0:T(8,128)(2,1)}, bf16[8,448,128]{2,1,0:T(8,128)(2,1)}, u32[]{:S(2)}, u32[]{:S(2)}) collective-permute-start(bf16[8,448,128]{2,1,0:T(8,128)(2,1)} %slice.548), channel_id=1, source_target_pairs={{2,0},{3,1},{4,2},{5,3},{6,4},{7,5},{8,6},{9,7},{10,8},{11,9},{12,... | collective-permute-start | bytes 2752520 | tf_op jit(solution)/shard_map/ppermute | solution.py:303
  358.5 268.2 %collective-permute-start.5 = (bf16[8,512,128]{2,1,0:T(8,128)(2,1)}, bf16[8,512,128]{2,1,0:T(8,128)(2,1)}, u32[]{:S(2)}, u32[]{:S(2)}) collective-permute-start(bf16[8,512,128]{2,1,0:T(8,128)(2,1)} %slice.549), channel_id=1, source_target_pairs={{1,0},{2,1},{3,2},{4,3},{5,4},{6,5},{7,6},{8,7},{9,8},{10,9},{11,1... | collective-permute-start | bytes 3145736 | tf_op jit(solution)/shard_map/ppermute | solution.py:303
  606.1 9.0 %copy-start.15 = (f32[512,128]{1,0:T(8,128)S(1)}, f32[512,128]{1,0:T(8,128)}, u32[]{:S(2)}) copy-start(f32[512,128]{1,0:T(8,128)} %get-tuple-element.121) | copy-start | bytes 786436
  614.0 4.1 copy-start.1
  620.0 1.7 copy-start.14
  620.0 2.7 copy-start.17
  620.0 3.7 copy-start.16
Sparse Core Ops, SparseCore 0:
  12.7 105.7 all-gather.4
  120.6 67.0 all-gather.6
  241.5 76.6 reduce-scatter.8
  336.0 124.2 reduce-scatter.10
  462.5 70.6 reduce-scatter.6
  535.4 70.7 reduce-scatter.4

commit v2 on v1

v2 whole, which is shorter than its diff:
```python
import functools

import jax
import jax.numpy as jnp
from jax import lax
from jax.experimental import pallas as pl
from jax.experimental.pallas import tpu as pltpu
from jax.sharding import PartitionSpec as P

BLOCK = 64
LOCAL = 16
STRIDE = 8
HALO = (LOCAL - 1) * BLOCK
ROWS = 256
CHUNK = 128
LOG2E = 1.4426950408889634
CHUNKS = (2, 3, 3)
F32 = jnp.float32
BF16 = jnp.bfloat16


def fold(x, op):
    rows, cols = x.shape
    return op(x.reshape(rows // 8, 8, cols), axis=0)


def pieces(total):
    return [(start, min(CHUNK, total - start)) for start in range(0, total, CHUNK)]


def attention_kernel(info_ref, q_ref, do_ref, ko_ref, vo_ref, k1_ref, v1_ref, k2_ref, v2_ref, kr1_ref, vr1_ref, kr2_ref, vr2_ref, ks_ref, vs_ref,
                     o_ref, dq_ref, own_ref, rest1_ref, rest2_ref, str_ref,
                     k_ext, v_ext, k_t, v_t, ks_t, vs_t, dk_acc, dv_acc, e_loc, e_str, pb_loc, pb_str, ds_loc, ds_str):
    shard = info_ref[1]
    head_idx, member = pl.program_id(0), pl.program_id(1)
    group_size = str_ref.shape[3]
    seq_loc, head_dim = q_ref.shape[2], q_ref.shape[3]
    n_res = seq_loc // BLOCK
    n_tiles = seq_loc // ROWS
    win = HALO + ROWS
    win_pad = pb_loc.shape[1]
    n_str = ks_t.shape[1]
    n_blk = n_str // BLOCK
    scale = 1.0 / head_dim
    to_exp2 = scale * LOG2E
    neg = -jnp.inf

    def res_of(slot):
        return lax.rem(STRIDE * 64 - 1 - ((info_ref[0] + head_idx) * group_size + slot), STRIDE)

    def rows_at(block):
        return pl.ds(pl.multiple_of(block * BLOCK, BLOCK), BLOCK)

    jres = res_of(member)

    @pl.when((head_idx == 0) & (member == 0))
    def _():
        for t in range(n_tiles):
            pb_loc[t, win:, :] = jnp.zeros((win_pad - win, ROWS), BF16)
            ds_loc[t, win:, :] = jnp.zeros((win_pad - win, ROWS), BF16)

    @pl.when(member == 0)
    def _():
        for ext, own, near, far, near_rest, far_rest in ((k_ext, ko_ref, k1_ref, k2_ref, kr1_ref, kr2_ref), (v_ext, vo_ref, v1_ref, v2_ref, vr1_ref, vr2_ref)):
            for slot in range(n_res):
                res = res_of(slot)
                far_blk = far[0, 0, 0, slot] if slot < group_size else far_rest[0, 0, slot - group_size]
                near_blk = near[0, 0, 0, slot] if slot < group_size else near_rest[0, 0, slot - group_size]
                ext[rows_at(res), :] = far_blk
                ext[rows_at(res + n_res), :] = near_blk
                ext[rows_at(res + 2 * n_res), :] = own[0, 0, slot]
        k_t[...] = jnp.zeros_like(k_t)
        v_t[...] = jnp.zeros_like(v_t)
        k_t[:, :HALO + seq_loc] = k_ext[BLOCK:, :].T
        v_t[:, :HALO + seq_loc] = v_ext[BLOCK:, :].T
        dk_acc[...] = jnp.zeros_like(dk_acc)
        dv_acc[...] = jnp.zeros_like(dv_acc)
        str_ref[n_blk:] = jnp.zeros((str_ref.shape[0] - n_blk,) + str_ref.shape[1:], F32)

    def str_rows(ref, start, size):
        return ref[start // BLOCK:(start + size) // BLOCK, 0, 0, 0].reshape(size, head_dim)

    def ext_rows(ref, start, size):
        return ref[BLOCK + start:BLOCK + start + size, :]

    ks_t[...] = str_rows(ks_ref, 0, n_str).T
    vs_t[...] = str_rows(vs_ref, 0, n_str).T

    y_row = lax.broadcasted_iota(jnp.int32, (1, ROWS), 1)
    st = [dict() for _ in range(n_tiles)]
    for t in range(n_tiles):
        st[t]['q_t'] = q_ref[0, 0, t * ROWS:(t + 1) * ROWS, :].T
        st[t]['do_t'] = do_ref[0, 0, t * ROWS:(t + 1) * ROWS, :].T
        st[t]['thr'] = shard - 1 - ((y_row // BLOCK + t * (ROWS // BLOCK)) < jres).astype(jnp.int32)

    def score_steps(t):
        s = st[t]

        def local(start, size):
            def run():
                sc = jnp.dot(ext_rows(k_ext, t * ROWS + start, size), s['q_t'], preferred_element_type=F32)
                for off in range(0, size, BLOCK):
                    x0 = start + off
                    sub = sc[off:off + BLOCK]
                    if x0 < HALO:
                        seen = t * ROWS + x0 >= HALO - seq_loc * shard
                        sub = sub + jnp.where(seen, 0.0, neg).astype(F32)
                    if x0 < ROWS - BLOCK:
                        sub = jnp.where(y_row < x0 + BLOCK, sub, neg)
                    if x0 >= HALO:
                        col = lax.broadcasted_iota(jnp.int32, (BLOCK, ROWS), 0)
                        row = lax.broadcasted_iota(jnp.int32, (BLOCK, ROWS), 1)
                        sub = jnp.where(col + (x0 - HALO) <= row, sub, neg)
                    e_loc[t, x0:x0 + BLOCK, :] = sub
                    part = fold(sub, jnp.max)
                    s['mx'] = part if 'mx' not in s else jnp.maximum(s['mx'], part)
            return run

        def strided(start, size):
            def run():
                sc = jnp.dot(str_rows(ks_ref, start, size), s['q_t'], preferred_element_type=F32)
                for off in range(0, size, BLOCK):
                    x0 = start + off
                    sub = sc[off:off + BLOCK] + jnp.where(x0 // BLOCK < s['thr'], 0.0, neg).astype(F32)
                    e_str[t, x0:x0 + BLOCK, :] = sub
                    s['mx'] = jnp.maximum(s['mx'], fold(sub, jnp.max))
            return run

        def finish():
            s['m'] = jnp.max(s['mx'], axis=0, keepdims=True)
        return [local(*p) for p in pieces(win)] + [strided(*p) for p in pieces(n_str)] + [finish]

    def exp_steps(t):
        s = st[t]

        def one(ref, start, size):
            def run():
                e = jnp.exp2((ref[t, start:start + size, :] - s['m']) * to_exp2)
                ref[t, start:start + size, :] = e
                part = fold(e, jnp.sum)
                s['l'] = part if 'l' not in s else s['l'] + part
            return run

        def finish():
            s['inv'] = 1.0 / jnp.sum(s['l'], axis=0, keepdims=True)
        return [one(e_loc, *p) for p in pieces(win)] + [one(e_str, *p) for p in pieces(n_str)] + [finish]

    def out_steps(t):
        s = st[t]

        def loc(start, size):
            def run():
                pb_loc[t, start:start + size, :] = (e_loc[t, start:start + size, :] * s['inv']).astype(BF16)
            return run

        def strided(start, size):
            def run():
                pb_str[start:start + size, t * ROWS:(t + 1) * ROWS] = (e_str[t, start:start + size, :] * s['inv']).astype(BF16)
            return run

        def finish():
            o_t = (jnp.dot(v_t[:, t * ROWS:t * ROWS + win_pad], pb_loc[t], preferred_element_type=F32)
                   + jnp.dot(vs_t[...], pb_str[:, t * ROWS:(t + 1) * ROWS], preferred_element_type=F32))
            s['delta'] = jnp.sum(s['do_t'].astype(F32) * o_t, axis=0, keepdims=True)
            o_ref[0, 0, t * ROWS:(t + 1) * ROWS, :] = o_t.T.astype(BF16)
        return [loc(*p) for p in pieces(win)] + [strided(*p) for p in pieces(n_str)] + [finish]

    def grad_steps(t):
        s = st[t]

        def loc(start, size):
            def run():
                dp = jnp.dot(ext_rows(v_ext, t * ROWS + start, size), s['do_t'], preferred_element_type=F32)
                p = e_loc[t, start:start + size, :] * s['inv']
                ds_loc[t, start:start + size, :] = (p * (dp - s['delta'])).astype(BF16)
            return run

        def strided(start, size):
            def run():
                dp = jnp.dot(str_rows(vs_ref, start, size), s['do_t'], preferred_element_type=F32)
                p = e_str[t, start:start + size, :] * s['inv']
                ds_str[start:start + size, t * ROWS:(t + 1) * ROWS] = (p * (dp - s['delta'])).astype(BF16)
            return run
        return [loc(*p) for p in pieces(win)] + [strided(*p) for p in pieces(n_str)]

    def back_steps(t):
        def dv():
            dv_acc[BLOCK + t * ROWS:BLOCK + t * ROWS + win, :] += jnp.dot(pb_loc[t, :win, :], do_ref[0, 0, t * ROWS:(t + 1) * ROWS, :], preferred_element_type=F32)

        def dk():
            dk_acc[BLOCK + t * ROWS:BLOCK + t * ROWS + win, :] += jnp.dot(ds_loc[t, :win, :], q_ref[0, 0, t * ROWS:(t + 1) * ROWS, :], preferred_element_type=F32)

        def dq():
            dq_t = (jnp.dot(k_t[:, t * ROWS:t * ROWS + win_pad], ds_loc[t], preferred_element_type=F32)
                    + jnp.dot(ks_t[...], ds_str[:, t * ROWS:(t + 1) * ROWS], preferred_element_type=F32))
            dq_ref[0, 0, t * ROWS:(t + 1) * ROWS, :] = (dq_t * scale).T.astype(BF16)
        return [dv, dk, dq]

    def weave(*lists):
        total = max(len(x) for x in lists)
        for i in range(total):
            for x in lists:
                for j in range(i * len(x) // total, (i + 1) * len(x) // total):
                    x[j]()

    weave(score_steps(0))
    for t in range(n_tiles):
        later = score_steps(t + 1) if t + 1 < n_tiles else []
        earlier = back_steps(t - 1) if t > 0 else []
        weave(*[x for x in (exp_steps(t), later, earlier) if x])
        weave(out_steps(t))
        weave(grad_steps(t))
    weave(back_steps(n_tiles - 1))

    str_ref[:n_blk, 1, 0, member] = jnp.dot(pb_str[...], do_ref[0, 0], preferred_element_type=F32).reshape(n_blk, BLOCK, head_dim)
    dks = jnp.dot(ds_str[...], q_ref[0, 0], preferred_element_type=F32) * scale
    str_ref[:n_blk, 0, 0, member] = dks.reshape(n_blk, BLOCK, head_dim)

    @pl.when(member == group_size - 1)
    def _():
        near_dev = jnp.maximum(shard - 1, 0)
        far_dev = jnp.maximum(shard - 2, 0)
        for w, acc, factor in ((0, dk_acc, scale), (1, dv_acc, 1.0)):
            for slot in range(n_res):
                res = res_of(slot)
                far = acc[rows_at(res), :] * factor
                near = acc[rows_at(res + n_res), :] * factor
                own_ref[w, 0, slot] = acc[rows_at(res + 2 * n_res), :] * factor
                if slot < group_size:
                    str_ref[far_dev, w, 0, slot] += far
                    str_ref[near_dev, w, 0, slot] += near
                else:
                    rest2_ref[w, 0, slot - group_size] = far.astype(BF16)
                    rest1_ref[w, 0, slot - group_size] = near.astype(BF16)


def attention(first_head, n_heads, shard, q, d_out, kv_rot, rest1, rest2, gathered):
    _, group_size, seq_loc, head_dim = q.shape
    n_res = seq_loc // BLOCK
    n_rest = n_res - group_size
    cp_size = gathered.shape[0]
    n_blk = cp_size - 2
    n_str = n_blk * BLOCK
    win = HALO + ROWS
    win_pad = -(-win // 256) * 256
    n_tiles = seq_loc // ROWS
    ext_len = BLOCK + HALO + seq_loc
    ext_pad = (n_tiles - 1) * ROWS + win_pad
    spec_q = pl.BlockSpec((1, 1, seq_loc, head_dim), lambda g, u, s: (s[0] + g, u, 0, 0))
    spec_o = pl.BlockSpec((1, 1, seq_loc, head_dim), lambda g, u, s: (g, u, 0, 0))
    own = [pl.BlockSpec((1, 1, n_res, BLOCK, head_dim), lambda g, u, s, w=w: (w, s[0] + g, 0, 0, 0)) for w in range(2)]
    prev = [[pl.BlockSpec((1, 1, 1, group_size, BLOCK, head_dim), lambda g, u, s, w=w, d=d: (jnp.maximum(s[1] - d, 0), w, g, 0, 0, 0)) for w in range(2)] for d in (1, 2)]
    rest = [pl.BlockSpec((1, 1, n_rest, BLOCK, head_dim), lambda g, u, s, w=w: (w, s[0] + g, 0, 0, 0)) for w in range(2)]
    strided = [pl.BlockSpec((n_blk, 1, 1, 1, BLOCK, head_dim), lambda g, u, s, w=w: (0, w, g, u, 0, 0)) for w in range(2)]
    spec_own = pl.BlockSpec((2, 1, n_res, BLOCK, head_dim), lambda g, u, s: (0, g, 0, 0, 0))
    spec_rest = pl.BlockSpec((2, 1, n_rest, BLOCK, head_dim), lambda g, u, s: (0, g, 0, 0, 0))
    spec_str = pl.BlockSpec((cp_size, 2, 1, group_size, BLOCK, head_dim), lambda g, u, s: (0, 0, g, 0, 0, 0))
    sds = jax.ShapeDtypeStruct
    flops = n_heads * group_size * 6 * 2 * seq_loc * (win + n_str) * head_dim
    info = jnp.stack([jnp.int32(first_head), shard.astype(jnp.int32)])
    return pl.pallas_call(
        attention_kernel,
        grid_spec=pltpu.PrefetchScalarGridSpec(
            num_scalar_prefetch=1,
            grid=(n_heads, group_size),
            in_specs=[spec_q, spec_q, *own, *prev[0], *prev[1], *rest, *rest, *strided],
            out_specs=[spec_o, spec_o, spec_own, spec_rest, spec_rest, spec_str],
            scratch_shapes=[
                pltpu.VMEM((ext_len, head_dim), BF16), pltpu.VMEM((ext_len, head_dim), BF16),
                pltpu.VMEM((head_dim, ext_pad), BF16), pltpu.VMEM((head_dim, ext_pad), BF16),
                pltpu.VMEM((head_dim, n_str), BF16), pltpu.VMEM((head_dim, n_str), BF16),
                pltpu.VMEM((ext_len, head_dim), F32), pltpu.VMEM((ext_len, head_dim), F32),
                pltpu.VMEM((n_tiles, win, ROWS), F32), pltpu.VMEM((n_tiles, n_str, ROWS), F32),
                pltpu.VMEM((n_tiles, win_pad, ROWS), BF16), pltpu.VMEM((n_str, seq_loc), BF16),
                pltpu.VMEM((n_tiles, win_pad, ROWS), BF16), pltpu.VMEM((n_str, seq_loc), BF16),
            ]),
        out_shape=[
            sds((n_heads, group_size, seq_loc, head_dim), BF16), sds((n_heads, group_size, seq_loc, head_dim), BF16),
            sds((2, n_heads, n_res, BLOCK, head_dim), F32),
            sds((2, n_heads, n_rest, BLOCK, head_dim), BF16), sds((2, n_heads, n_rest, BLOCK, head_dim), BF16),
            sds((cp_size, 2, n_heads, group_size, BLOCK, head_dim), F32),
        ],
        compiler_params=pltpu.CompilerParams(vmem_limit_bytes=56 * 1024 * 1024),
        cost_estimate=pl.CostEstimate(flops=flops, bytes_accessed=0, transcendentals=0),
        name='attention',
    )(info, q, d_out, kv_rot, kv_rot, gathered, gathered, gathered, gathered, rest1, rest1, rest2, rest2, gathered, gathered)


def rotate_kernel(group_size, k_ref, v_ref, out_ref):
    n_res = out_ref.shape[2]
    for w, ref in enumerate((k_ref, v_ref)):
        for slot in range(n_res):
            res = lax.rem(STRIDE * 64 - 1 - (pl.program_id(0) * group_size + slot), STRIDE)
            out_ref[w, 0, slot] = ref[0, pl.ds(pl.multiple_of(res * BLOCK, BLOCK), BLOCK), :]


def rotate(k_h, v_h, group_size):
    kv_heads, seq_loc, head_dim = k_h.shape
    n_res = seq_loc // BLOCK
    spec = pl.BlockSpec((1, seq_loc, head_dim), lambda g: (g, 0, 0))
    return pl.pallas_call(
        functools.partial(rotate_kernel, group_size),
        grid=(kv_heads,),
        in_specs=[spec, spec],
        out_specs=pl.BlockSpec((2, 1, n_res, BLOCK, head_dim), lambda g: (0, g, 0, 0, 0)),
        out_shape=jax.ShapeDtypeStruct((2, kv_heads, n_res, BLOCK, head_dim), BF16),
        cost_estimate=pl.CostEstimate(flops=10 ** 7, bytes_accessed=0, transcendentals=0),
        name='rotate',
    )(k_h, v_h)


def merge_kernel(first_head, own_ref, red_ref, back1_ref, back2_ref, out_ref):
    n_res, group_size = own_ref.shape[2], red_ref.shape[2]
    for w in range(2):
        for slot in range(n_res):
            res = lax.rem(STRIDE * 64 - 1 - ((first_head + pl.program_id(0)) * group_size + slot), STRIDE)
            if slot < group_size:
                total = own_ref[w, 0, slot] + red_ref[w, 0, slot]
            else:
                total = own_ref[w, 0, slot] + back1_ref[w, 0, slot - group_size].astype(F32) + back2_ref[w, 0, slot - group_size].astype(F32)
            out_ref[w, 0, pl.ds(pl.multiple_of(res * BLOCK, BLOCK), BLOCK), :] = total.astype(BF16)


def merge(first_head, own, reduced, back1, back2):
    _, n_heads, n_res, _, head_dim = own.shape
    group_size, n_rest = reduced.shape[2], back1.shape[2]
    seq_loc = n_res * BLOCK

    def spec(count):
        return pl.BlockSpec((2, 1, count, BLOCK, head_dim), lambda g: (0, g, 0, 0, 0))
    return pl.pallas_call(
        functools.partial(merge_kernel, first_head),
        grid=(n_heads,),
        in_specs=[spec(n_res), spec(group_size), spec(n_rest), spec(n_rest)],
        out_specs=pl.BlockSpec((2, 1, seq_loc, head_dim), lambda g: (0, g, 0, 0)),
        out_shape=jax.ShapeDtypeStruct((2, n_heads, seq_loc, head_dim), BF16),
        cost_estimate=pl.CostEstimate(flops=10 ** 7, bytes_accessed=0, transcendentals=0),
        name='merge',
    )(own, reduced, back1, back2)


def solution(mesh):
    cp_size = mesh.shape['cp']
    spec = P('dp', 'cp', None, None)

    def per_device(q_rope, k_rope, values, d_out):
        seq_loc, heads, head_dim = q_rope.shape[1:]
        kv_heads = k_rope.shape[2]
        group_size = heads // kv_heads
        shard = lax.axis_index('cp')
        kv_rot = rotate(jnp.swapaxes(k_rope[0], 0, 1), jnp.swapaxes(values[0], 0, 1), group_size)
        starts = [sum(CHUNKS[:i]) for i in range(len(CHUNKS))]
        gathered = [lax.all_gather(kv_rot[:, a:a + n, :group_size], 'cp', axis=0, tiled=False) for a, n in zip(starts, CHUNKS)]
        rest = kv_rot[:, :, group_size:]
        rest1, rest2 = [lax.ppermute(rest, 'cp', [(s, s + dist) for s in range(cp_size - dist)]) for dist in (1, 2)]

        def head_major(x):
            return jnp.transpose(x[0].reshape(seq_loc, kv_heads, group_size, head_dim), (1, 2, 0, 3))

        q_h, do_h = head_major(q_rope), head_major(d_out)
        outs = [attention(a, n, shard, q_h, do_h, kv_rot, rest1, rest2, gathered[i]) for i, (a, n) in enumerate(zip(starts, CHUNKS))]
        reduced = [lax.psum_scatter(out[5], 'cp', scatter_dimension=0, tiled=False) for out in outs]

        def token_major(xs):
            x = jnp.concatenate(xs, axis=0)
            return jnp.transpose(x, (2, 0, 1, 3)).reshape(1, seq_loc, heads, head_dim)

        attn_out = token_major([out[0] for out in outs])
        d_q = token_major([out[1] for out in outs])

        merged = []
        for i, (out, red) in enumerate(zip(outs, reduced)):
            back = [lax.ppermute(out[2 + dist], 'cp', [(s + dist, s) for s in range(cp_size - dist)]) for dist in (1, 2)]
            merged.append(merge(starts[i], out[2], red, back[0], back[1]))
        plain = jnp.swapaxes(jnp.concatenate(merged, axis=1), 1, 2)
        return attn_out, d_q, plain[0][None], plain[1][None]

    return jax.shard_map(per_device, mesh=mesh, in_specs=(spec, spec, spec, spec), out_specs=(spec, spec, spec, spec), check_vma=False)
```

time: 641 us -> 482 us (0.75)
  waiting for transfers between devices: 310 us -> 193 us
  local copies, waits for them, and re-layouts: 101 us -> 33.3 us
  Pallas kernels: 181 us -> 213 us
  other arithmetic: 13.8 us -> 6.83 us
    ppermute x6 -> x8, waiting for transfers between devices: 97.1 us -> 36.1 us  [the longest x2 36.1 us: per_device(): lax.ppermute(rest, 'cp', [(s, s + dist) for s in range(cp_size - dist)])]
    reduce_scatter x4 -> x3, waiting for transfers between devices: 211 us -> 153 us  [per_device(): lax.psum_scatter(out[5], 'cp', scatter_dimension=0, tiled=False)]
    unnamed x99 -> x32, local copies, waits for them, and re-layouts: 77.6 us -> 24.6 us
    pallas_call x2 -> x7, Pallas kernels: 181 us -> 213 us  [the longest x3 198 us: attention(): pl.pallas_call(attention_kernel, grid_spec=pltpu.PrefetchScalarGridSpec(n...]
    all_gather x1 -> x0, local copies, waits for them, and re-layouts: 11.7 us -> none  [per_device(): lax.all_gather(kv_c[:, i * per:(i + 1) * per], 'cp', axis=0, tiled=False)]
    concatenate x1 -> x0, other arithmetic: 6.75 us -> none  [per_device(): jnp.concatenate(parts + [kv, jnp.zeros((2, kv_heads, pad, head_dim), BF16...]
    ppermute x6 -> x8, starting transfers between devices: 16.2 us -> 19.6 us  [the longest x6 10.6 us: per_device(): lax.ppermute(out[2 + dist], 'cp', [(s + dist, s) for s in range(cp_size -...]
  transfers between devices with their start and end apart: 12 -> 14, of which waited for: 4 -> 5; matrix products, arithmetic and copies ran while one was open for 16% -> 6% of each run, Pallas kernels for 28% -> 42%
where the time goes in v2:
time: 482 us; the launch traced here: 481 us
  Pallas kernels  213 us (44%)
  waiting for transfers between devices  193 us (40%)
  local copies, waits for them, and re-layouts  33.3 us (7%)
  starting transfers between devices  20.2 us (4%)
  between operations  14.4 us (3%)
  other arithmetic  6.83 us (1%)
    pallas_call x3, Pallas kernels, attention(): pl.pallas_call(attention_kernel, grid_spec=pltpu.PrefetchScalarGridSpec(n...  198 us
    reduce_scatter x3, waiting for transfers between devices, per_device(): lax.psum_scatter(out[5], 'cp', scatter_dimension=0, tiled=False)  153 us
    ppermute x2, waiting for transfers between devices, per_device(): lax.ppermute(rest, 'cp', [(s, s + dist) for s in range(cp_size - dist)])  36.1 us
    unnamed x32, local copies, waits for them, and re-layouts  24.6 us
    ppermute x6, starting transfers between devices, per_device(): lax.ppermute(out[2 + dist], 'cp', [(s + dist, s) for s in range(cp_size -...  10.6 us
  transfers between devices with their start and end apart: 14, of which 5 were waited for; matrix products, arithmetic and copies ran while one was open for 6% of the time, Pallas kernels for 42%

profile of v2, /device:TPU:21, one launch (start us, length us, event | category | flops | bytes accessed | tf_op | source)
XLA Modules:
  0.0 480.7 jit_solution(13916038036612246444)
XLA Ops:
  7.2 0.1 all-gather.7.cloned.1.call-start
  7.2 3.2 copy_bitcast_fusion
  10.5 5.7 %rotate.1.ko_ref.vo_ref = bf16[2,8,8,64,128]{4,3,2,1,0:T(8,128)(2,1)} custom-call(bf16[8,512,128]{2,1,0:T(8,128)(2,1)} %get-tuple-element.53.k_ref, bf16[8,512,128]{2,1,0:T(8,128)(2,1)} %get-tuple-element.52.v_ref), custom_call_target="tpu_custom_call" | custom-call | flops 10000000 | tf_op jit(solution)/shard_map/rotate/pallas_call | solution.py:301
  16.2 1.7 slice.24
  17.9 0.1 all-gather.7.cloned.1.call-update
  18.0 0.1 all-gather.9.cloned.1.call-start
  18.1 2.2 fusion.1
  20.3 0.1 all-gather.9.cloned.1.call-update
  20.3 0.1 all-gather.11.cloned.1.call-start
  20.4 0.7 all-gather.11.cloned.1.call-update
  21.1 0.1 reduce-scatter.4.cloned.1.call-start
  21.2 0.0 slice-start
  21.2 1.3 slice.25
  22.5 5.2 %collective-permute-start = (bf16[2,8,3,64,128]{4,3,2,1,0:T(8,128)(2,1)S(1)}, bf16[2,8,3,64,128]{4,3,2,1,0:T(8,128)(2,1)S(1)}, u32[]{:S(2)}, u32[]{:S(2)}) collective-permute-start(bf16[2,8,3,64,128]{4,3,2,1,0:T(8,128)(2,1)S(1)} %slice.25), channel_id=1, source_target_pairs={{0,1},{1,2},{2,3},{3,4},{4,5},{5,6},{6,7},{7,8},{8,9},{9,10},{10,1... | collective-permute-start | bytes 2359304 | tf_op jit(solution)/shard_map/ppermute | solution.py:355
  27.8 3.8 collective-permute-start.1
  31.6 0.0 slice-start.1
  31.6 6.2 %copy.16 = bf16[1,512,40,128]{3,1,2,0:T(8,128)(2,1)} copy(bf16[1,512,40,128]{3,2,1,0:T(8,128)(2,1)} %param.4) | data formatting | bytes 10485760 | tf_op args[0]
  37.8 3.6 copy.17
  41.5 0.6 pad_add_fusion.info_ref
  42.0 11.8 %collective-permute-done.kr1_ref.vr1_ref = bf16[2,8,3,64,128]{4,3,2,1,0:T(8,128)(2,1)S(1)} collective-permute-done((bf16[2,8,3,64,128]{4,3,2,1,0:T(8,128)(2,1)S(1)}, bf16[2,8,3,64,128]{4,3,2,1,0:T(8,128)(2,1)S(1)}, u32[]{:S(2)}, u32[]{:S(2)}) %collective-permute-start) | collective-permute-done | bytes 786464 | tf_op jit(solution)/shard_map/ppermute | solution.py:355
  53.9 24.2 %collective-permute-done.1.kr2_ref.vr2_ref = bf16[2,8,3,64,128]{4,3,2,1,0:T(8,128)(2,1)S(1)} collective-permute-done((bf16[2,8,3,64,128]{4,3,2,1,0:T(8,128)(2,1)S(1)}, bf16[2,8,3,64,128]{4,3,2,1,0:T(8,128)(2,1)S(1)}, u32[]{:S(2)}, u32[]{:S(2)}) %collective-permute-start.1) | collective-permute-done | bytes 786464 | tf_op jit(solution)/shard_map/ppermute | solution.py:355
  78.1 2.4 all-gather.7.cloned.1.call-done
  80.5 0.0 copy-done.9
  80.5 50.7 %attention.3 = (bf16[2,5,512,128]{3,2,1,0:T(8,128)(2,1)}, bf16[2,5,512,128]{3,2,1,0:T(8,128)(2,1)}, f32[2,2,8,64,128]{4,3,2,1,0:T(8,128)}, bf16[2,2,3,64,128]{4,...) custom-call(s32[2]{0:T(128)} %pad_add_fusion.info_ref, ...), custom_call_target="tpu_custom_call" | custom-call | flops 16609443840 | tf_op jit(solution)/shard_map/attention/pallas_call | solution.py:261
  131.3 0.1 reduce-scatter.4.cloned.1.call-update
  131.3 0.2 reduce-scatter.6.cloned.1.call-start
  131.6 0.6 pad_add_fusion.1.info_ref
  132.2 73.9 %attention.4 = (bf16[3,5,512,128]{3,2,1,0:T(8,128)(2,1)}, bf16[3,5,512,128]{3,2,1,0:T(8,128)(2,1)}, f32[2,3,8,64,128]{4,3,2,1,0:T(8,128)}, bf16[2,3,3,64,128]{4,...) custom-call(s32[2]{0:T(128)} %pad_add_fusion.1.info_ref, ...), custom_call_target="tpu_custom_call" | custom-call | flops 24914165760 | tf_op jit(solution)/shard_map/attention/pallas_call | solution.py:261
  206.0 0.1 reduce-scatter.6.cloned.1.call-update
  206.1 0.1 reduce-scatter.8.cloned.1.call-start
  206.2 0.6 pad_add_fusion.2.info_ref
  206.8 73.8 %attention.5 = (bf16[3,5,512,128]{3,2,1,0:T(8,128)(2,1)}, bf16[3,5,512,128]{3,2,1,0:T(8,128)(2,1)}, f32[2,3,8,64,128]{4,3,2,1,0:T(8,128)}, bf16[2,3,3,64,128]{4,...) custom-call(s32[2]{0:T(128)} %pad_add_fusion.2.info_ref, ...), custom_call_target="tpu_custom_call" | custom-call | flops 24914165760 | tf_op jit(solution)/shard_map/attention/pallas_call | solution.py:261
  280.6 0.1 reduce-scatter.8.cloned.1.call-update
  280.7 2.5 collective-permute-start.2
  283.2 1.3 collective-permute-start.3
  284.6 2.0 collective-permute-start.4
  286.5 1.3 collective-permute-start.5
  287.8 2.2 collective-permute-start.6
  290.0 0.0 copy-done.2
  290.0 0.0 copy-done.5
  290.0 2.7 pad_maximum_fusion.1
  292.7 0.0 copy-start.10
  292.7 0.0 copy-start.1
  292.7 0.0 copy-start.3
  292.7 0.0 copy-start.4
  292.7 5.7 %copy.21 = bf16[1,512,40,128]{3,2,1,0:T(8,128)(2,1)} copy(bf16[1,512,40,128]{3,1,2,0:T(8,128)(2,1)S(1)} %bitcast.29) | data formatting | bytes 10485760
  298.5 0.0 collective-permute-done.2.back1_ref
  298.5 1.3 collective-permute-start.7
  299.8 0.8 pad_maximum_fusion
  300.6 5.7 %copy.20 = bf16[1,512,40,128]{3,2,1,0:T(8,128)(2,1)} copy(bf16[1,512,40,128]{3,1,2,0:T(8,128)(2,1)S(1)} %bitcast.30) | data formatting | bytes 10485760
  306.4 0.0 collective-permute-done.3.back2_ref
  306.4 2.3 merge.3
  308.7 0.0 collective-permute-done.4.back1_ref
  308.7 0.0 collective-permute-done.5.back2_ref
  308.7 63.2 %reduce-scatter.6.cloned.1.call-done = f32[1,2,3,5,64,128]{5,4,3,2,1,0:T(8,128)} async-done(((f32[16,2,3,5,64,128]{5,4,3,2,1,0:T(8,128)}), f32[1,2,3,5,64,128]{5,4,3,2,1,0:T(8,128)}) %reduce-scatter.6.cloned.1.call-update) | async-done | bytes 983056 | tf_op jit(solution)/shard_map/reduce_scatter | solution.py:362
  371.9 3.5 merge.4
  375.4 0.0 collective-permute-done.6.back1_ref
  375.4 0.0 collective-permute-done.7.back2_ref
  375.4 90.0 %reduce-scatter.8.cloned.1.call-done = f32[1,2,3,5,64,128]{5,4,3,2,1,0:T(8,128)} async-done(((f32[16,2,3,5,64,128]{5,4,3,2,1,0:T(8,128)}), f32[1,2,3,5,64,128]{5,4,3,2,1,0:T(8,128)}) %reduce-scatter.8.cloned.1.call-update) | async-done | bytes 983056 | tf_op jit(solution)/shard_map/reduce_scatter | solution.py:362
  465.4 3.5 merge.5
  468.8 1.6 maximum_bitcast_fusion
  470.4 0.1 fusion
  470.6 1.6 copy.22
  472.2 1.6 copy.23
  (21 shorter events, 0.0 us)
Async XLA Ops:
  7.2 73.3 %all-gather.7.cloned.1.call-start = ((), (), s32[]{:S(2)}) async-start(), calls=%async_computation.6 | async-start | bytes 5570560 | tf_op jit(solution)/shard_map/all_gather | solution.py:353
  18.0 114.2 %all-gather.9.cloned.1.call-start = ((), (), s32[]{:S(2)}) async-start(), calls=%async_computation.7 | async-start | bytes 8355840 | tf_op jit(solution)/shard_map/all_gather | solution.py:353
  20.3 186.5 %all-gather.11.cloned.1.call-start = ((), (), s32[]{:S(2)}) async-start(), calls=%async_computation.8 | async-start | bytes 8355840 | tf_op jit(solution)/shard_map/all_gather | solution.py:353
  21.1 285.3 %reduce-scatter.4.cloned.1.call-start = ((), (), s32[]{:S(2)}) async-start(), calls=%async_computation.3 | async-start | bytes 11141120 | tf_op jit(solution)/shard_map/reduce_scatter | solution.py:362
  21.2 16.6 %slice-start = ((s8[5242880]{0:T(1024)(128)(4,1)}), s8[4194304]{0:T(1024)(128)(4,1)S(1)}, s32[]{:S(2)}) async-start(s8[5242880]{0:T(1024)(128)(4,1)} %bitcast.31), calls=%async_computation.9 | async-start | bytes 8388608
  22.5 31.3 %collective-permute-start = (bf16[2,8,3,64,128]{4,3,2,1,0:T(8,128)(2,1)S(1)}, bf16[2,8,3,64,128]{4,3,2,1,0:T(8,128)(2,1)S(1)}, u32[]{:S(2)}, u32[]{:S(2)}) collective-permute-start(bf16[2,8,3,64,128]{4,3,2,1,0:T(8,128)(2,1)S(1)} %slice.25), channel_id=1, source_target_pairs={{0,1},{1,2},{2,3},{3,4},{4,5},{5,6},{6,7},{7,8},{8,9},{9,10},{10,1... | collective-permute-start | bytes 2359304 | tf_op jit(solution)/shard_map/ppermute | solution.py:355
  27.8 50.3 %collective-permute-start.1 = (bf16[2,8,3,64,128]{4,3,2,1,0:T(8,128)(2,1)S(1)}, bf16[2,8,3,64,128]{4,3,2,1,0:T(8,128)(2,1)S(1)}, u32[]{:S(2)}, u32[]{:S(2)}) collective-permute-start(bf16[2,8,3,64,128]{4,3,2,1,0:T(8,128)(2,1)S(1)} %slice.25), channel_id=1, source_target_pairs={{0,2},{1,3},{2,4},{3,5},{4,6},{5,7},{6,8},{7,9},{8,10},{9,11},{10,... | collective-permute-start | bytes 2359304 | tf_op jit(solution)/shard_map/ppermute | solution.py:355
  31.6 6.2 %slice-start.1 = ((s8[5242880]{0:T(1024)(128)(4,1)}), s8[1048576]{0:T(1024)(128)(4,1)S(1)}, s32[]{:S(2)}) async-start(s8[5242880]{0:T(1024)(128)(4,1)} %bitcast.31), calls=%async_computation.10 | async-start | bytes 2097152
  53.9 26.7 %copy-start.8 = (bf16[2,8,3,64,128]{4,3,2,1,0:T(8,128)(2,1)}, bf16[2,8,3,64,128]{4,3,2,1,0:T(8,128)(2,1)S(1)}, u32[]{:S(2)}) copy-start(bf16[2,8,3,64,128]{4,3,2,1,0:T(8,128)(2,1)S(1)} %collective-permute-done.kr1_ref.vr1_ref) | copy-start | bytes 2359300
  78.1 2.4 copy-start.9
  131.3 240.6 %reduce-scatter.6.cloned.1.call-start = ((), (), s32[]{:S(2)}) async-start(), calls=%async_computation.4 | async-start | bytes 16711680 | tf_op jit(solution)/shard_map/reduce_scatter | solution.py:362
  206.1 259.3 %reduce-scatter.8.cloned.1.call-start = ((), (), s32[]{:S(2)}) async-start(), calls=%async_computation.5 | async-start | bytes 16711680 | tf_op jit(solution)/shard_map/reduce_scatter | solution.py:362
  280.6 9.4 %copy-start.2 = (bf16[3,5,512,128]{3,2,1,0:T(8,128)(2,1)S(1)}, bf16[3,5,512,128]{3,2,1,0:T(8,128)(2,1)}, u32[]{:S(2)}) copy-start(bf16[3,5,512,128]{3,2,1,0:T(8,128)(2,1)} %get-tuple-element.26) | copy-start | bytes 5898244
  280.6 9.4 %copy-start.5 = (bf16[2,5,512,128]{3,2,1,0:T(8,128)(2,1)S(1)}, bf16[2,5,512,128]{3,2,1,0:T(8,128)(2,1)}, u32[]{:S(2)}) copy-start(bf16[2,5,512,128]{3,2,1,0:T(8,128)(2,1)} %get-tuple-element.25) | copy-start | bytes 3932164
  280.7 17.8 %collective-permute-start.2 = (bf16[2,2,3,64,128]{4,3,2,1,0:T(8,128)(2,1)}, bf16[2,2,3,64,128]{4,3,2,1,0:T(8,128)(2,1)S(1)}, u32[]{:S(2)}, u32[]{:S(2)}) collective-permute-start(bf16[2,2,3,64,128]{4,3,2,1,0:T(8,128)(2,1)} %get-tuple-element.30), channel_id=1, source_target_pairs={{1,0},{2,1},{3,2},{4,3},{5,4},{6,5},{7,6},{8,7},{9,8},{10,9},{11,1... | collective-permute-start | bytes 589832 | tf_op jit(solution)/shard_map/ppermute | solution.py:373
  283.2 23.1 %collective-permute-start.3 = (bf16[2,2,3,64,128]{4,3,2,1,0:T(8,128)(2,1)}, bf16[2,2,3,64,128]{4,3,2,1,0:T(8,128)(2,1)}, u32[]{:S(2)}, u32[]{:S(2)}) collective-permute-start(bf16[2,2,3,64,128]{4,3,2,1,0:T(8,128)(2,1)} %get-tuple-element.31), channel_id=1, source_target_pairs={{2,0},{3,1},{4,2},{5,3},{6,4},{7,5},{8,6},{9,7},{10,8},{11,9},{12,... | collective-permute-start | bytes 589832 | tf_op jit(solution)/shard_map/ppermute | solution.py:373
  284.6 24.1 %collective-permute-start.4 = (bf16[2,3,3,64,128]{4,3,2,1,0:T(8,128)(2,1)}, bf16[2,3,3,64,128]{4,3,2,1,0:T(8,128)(2,1)}, u32[]{:S(2)}, u32[]{:S(2)}) collective-permute-start(bf16[2,3,3,64,128]{4,3,2,1,0:T(8,128)(2,1)} %get-tuple-element.34), channel_id=1, source_target_pairs={{1,0},{2,1},{3,2},{4,3},{5,4},{6,5},{7,6},{8,7},{9,8},{10,9},{11,1... | collective-permute-start | bytes 884744 | tf_op jit(solution)/shard_map/ppermute | solution.py:373
  286.5 22.1 %collective-permute-start.5 = (bf16[2,3,3,64,128]{4,3,2,1,0:T(8,128)(2,1)}, bf16[2,3,3,64,128]{4,3,2,1,0:T(8,128)(2,1)}, u32[]{:S(2)}, u32[]{:S(2)}) collective-permute-start(bf16[2,3,3,64,128]{4,3,2,1,0:T(8,128)(2,1)} %get-tuple-element.35), channel_id=1, source_target_pairs={{2,0},{3,1},{4,2},{5,3},{6,4},{7,5},{8,6},{9,7},{10,8},{11,9},{12,... | collective-permute-start | bytes 884744 | tf_op jit(solution)/shard_map/ppermute | solution.py:373
  287.8 87.5 %collective-permute-start.6 = (bf16[2,3,3,64,128]{4,3,2,1,0:T(8,128)(2,1)}, bf16[2,3,3,64,128]{4,3,2,1,0:T(8,128)(2,1)}, u32[]{:S(2)}, u32[]{:S(2)}) collective-permute-start(bf16[2,3,3,64,128]{4,3,2,1,0:T(8,128)(2,1)} %get-tuple-element.38), channel_id=1, source_target_pairs={{1,0},{2,1},{3,2},{4,3},{5,4},{6,5},{7,6},{8,7},{9,8},{10,9},{11,1... | collective-permute-start | bytes 884744 | tf_op jit(solution)/shard_map/ppermute | solution.py:373
  292.7 5.8 %copy-start.10 = (bf16[2,3,3,64,128]{4,3,2,1,0:T(8,128)(2,1)S(1)}, bf16[2,3,3,64,128]{4,3,2,1,0:T(8,128)(2,1)}, u32[]{:S(2)}) copy-start(bf16[2,3,3,64,128]{4,3,2,1,0:T(8,128)(2,1)} %get-tuple-element.39) | copy-start | bytes 884740
  292.7 7.1 %copy-start.1 = (bf16[3,5,512,128]{3,2,1,0:T(8,128)(2,1)S(1)}, bf16[3,5,512,128]{3,2,1,0:T(8,128)(2,1)}, u32[]{:S(2)}) copy-start(bf16[3,5,512,128]{3,2,1,0:T(8,128)(2,1)} %get-tuple-element.23) | copy-start | bytes 5898244
  292.7 7.1 %copy-start.3 = (bf16[3,5,512,128]{3,2,1,0:T(8,128)(2,1)S(1)}, bf16[3,5,512,128]{3,2,1,0:T(8,128)(2,1)}, u32[]{:S(2)}) copy-start(bf16[3,5,512,128]{3,2,1,0:T(8,128)(2,1)} %get-tuple-element.24) | copy-start | bytes 5898244
  292.7 7.1 %copy-start.4 = (bf16[2,5,512,128]{3,2,1,0:T(8,128)(2,1)S(1)}, bf16[2,5,512,128]{3,2,1,0:T(8,128)(2,1)}, u32[]{:S(2)}) copy-start(bf16[2,5,512,128]{3,2,1,0:T(8,128)(2,1)} %get-tuple-element.22) | copy-start | bytes 3932164
  298.5 2.1 copy-start.7
  298.5 76.9 %collective-permute-start.7 = (bf16[2,3,3,64,128]{4,3,2,1,0:T(8,128)(2,1)S(1)}, bf16[2,3,3,64,128]{4,3,2,1,0:T(8,128)(2,1)S(1)}, u32[]{:S(2)}, u32[]{:S(2)}) collective-permute-start(bf16[2,3,3,64,128]{4,3,2,1,0:T(8,128)(2,1)S(1)} %copy-done.10), channel_id=1, source_target_pairs={{2,0},{3,1},{4,2},{5,3},{6,4},{7,5},{8,6},{9,7},{10,8},{11,9},{12,... | collective-permute-start | bytes 884744 | tf_op jit(solution)/shard_map/ppermute | solution.py:373
  308.7 160.2 %copy-start = (bf16[2,2,512,128]{3,2,1,0:T(8,128)(2,1)S(1)}, bf16[2,2,512,128]{3,2,1,0:T(8,128)(2,1)}, u32[]{:S(2)}) copy-start(bf16[2,2,512,128]{3,2,1,0:T(8,128)(2,1)} %merge.3) | copy-start | bytes 1572868
  375.4 90.0 %copy-start.6 = (bf16[2,3,3,64,128]{4,3,2,1,0:T(8,128)(2,1)}, bf16[2,3,3,64,128]{4,3,2,1,0:T(8,128)(2,1)S(1)}, u32[]{:S(2)}) copy-start(bf16[2,3,3,64,128]{4,3,2,1,0:T(8,128)(2,1)S(1)} %collective-permute-done.7.back2_ref) | copy-start | bytes 884740
Sparse Core Ops, SparseCore 0:
  18.1 62.3 all-gather.6
  82.2 49.8 all-gather.8
  133.7 48.5 all-gather.10
  184.5 66.8 reduce-scatter.3
  253.6 118.2 reduce-scatter.5
  374.1 91.1 reduce-scatter.7

commit v3 on v2

--- a/solution.py
+++ b/solution.py
@@ -248,9 +248,9 @@
     ext_pad = (n_tiles - 1) * ROWS + win_pad
     spec_q = pl.BlockSpec((1, 1, seq_loc, head_dim), lambda g, u, s: (s[0] + g, u, 0, 0))
     spec_o = pl.BlockSpec((1, 1, seq_loc, head_dim), lambda g, u, s: (g, u, 0, 0))
-    own = [pl.BlockSpec((1, 1, n_res, BLOCK, head_dim), lambda g, u, s, w=w: (w, s[0] + g, 0, 0, 0)) for w in range(2)]
+    own = [pl.BlockSpec((1, 1, n_res, BLOCK, head_dim), lambda g, u, s, w=w: (w, g, 0, 0, 0)) for w in range(2)]
     prev = [[pl.BlockSpec((1, 1, 1, group_size, BLOCK, head_dim), lambda g, u, s, w=w, d=d: (jnp.maximum(s[1] - d, 0), w, g, 0, 0, 0)) for w in range(2)] for d in (1, 2)]
-    rest = [pl.BlockSpec((1, 1, n_rest, BLOCK, head_dim), lambda g, u, s, w=w: (w, s[0] + g, 0, 0, 0)) for w in range(2)]
+    rest = [pl.BlockSpec((1, 1, n_rest, BLOCK, head_dim), lambda g, u, s, w=w: (w, g, 0, 0, 0)) for w in range(2)]
     strided = [pl.BlockSpec((n_blk, 1, 1, 1, BLOCK, head_dim), lambda g, u, s, w=w: (0, w, g, u, 0, 0)) for w in range(2)]
     spec_own = pl.BlockSpec((2, 1, n_res, BLOCK, head_dim), lambda g, u, s: (0, g, 0, 0, 0))
     spec_rest = pl.BlockSpec((2, 1, n_rest, BLOCK, head_dim), lambda g, u, s: (0, g, 0, 0, 0))
@@ -286,24 +286,24 @@
     )(info, q, d_out, kv_rot, kv_rot, gathered, gathered, gathered, gathered, rest1, rest1, rest2, rest2, gathered, gathered)
 
 
-def rotate_kernel(group_size, k_ref, v_ref, out_ref):
+def rotate_kernel(first_head, group_size, k_ref, v_ref, out_ref):
     n_res = out_ref.shape[2]
     for w, ref in enumerate((k_ref, v_ref)):
         for slot in range(n_res):
-            res = lax.rem(STRIDE * 64 - 1 - (pl.program_id(0) * group_size + slot), STRIDE)
+            res = lax.rem(STRIDE * 64 - 1 - ((first_head + pl.program_id(0)) * group_size + slot), STRIDE)
             out_ref[w, 0, slot] = ref[0, pl.ds(pl.multiple_of(res * BLOCK, BLOCK), BLOCK), :]
 
 
-def rotate(k_h, v_h, group_size):
-    kv_heads, seq_loc, head_dim = k_h.shape
+def rotate(first_head, n_heads, k_h, v_h, group_size):
+    _, seq_loc, head_dim = k_h.shape
     n_res = seq_loc // BLOCK
-    spec = pl.BlockSpec((1, seq_loc, head_dim), lambda g: (g, 0, 0))
+    spec = pl.BlockSpec((1, seq_loc, head_dim), lambda g: (first_head + g, 0, 0))
     return pl.pallas_call(
-        functools.partial(rotate_kernel, group_size),
-        grid=(kv_heads,),
+        functools.partial(rotate_kernel, first_head, group_size),
+        grid=(n_heads,),
         in_specs=[spec, spec],
         out_specs=pl.BlockSpec((2, 1, n_res, BLOCK, head_dim), lambda g: (0, g, 0, 0, 0)),
-        out_shape=jax.ShapeDtypeStruct((2, kv_heads, n_res, BLOCK, head_dim), BF16),
+        out_shape=jax.ShapeDtypeStruct((2, n_heads, n_res, BLOCK, head_dim), BF16),
         cost_estimate=pl.CostEstimate(flops=10 ** 7, bytes_accessed=0, transcendentals=0),
         name='rotate',
     )(k_h, v_h)
@@ -348,17 +348,22 @@
         kv_heads = k_rope.shape[2]
         group_size = heads // kv_heads
         shard = lax.axis_index('cp')
-        kv_rot = rotate(jnp.swapaxes(k_rope[0], 0, 1), jnp.swapaxes(values[0], 0, 1), group_size)
         starts = [sum(CHUNKS[:i]) for i in range(len(CHUNKS))]
-        gathered = [lax.all_gather(kv_rot[:, a:a + n, :group_size], 'cp', axis=0, tiled=False) for a, n in zip(starts, CHUNKS)]
-        rest = kv_rot[:, :, group_size:]
-        rest1, rest2 = [lax.ppermute(rest, 'cp', [(s, s + dist) for s in range(cp_size - dist)]) for dist in (1, 2)]
+        k_h, v_h = jnp.swapaxes(k_rope[0], 0, 1), jnp.swapaxes(values[0], 0, 1)
+
+        def onward(x):
+            return lax.ppermute(x, 'cp', [(s, s + 1) for s in range(cp_size - 1)])
+
+        kv_rot = [rotate(a, n, k_h, v_h, group_size) for a, n in zip(starts, CHUNKS)]
+        gathered = [lax.all_gather(x[:, :, :group_size], 'cp', axis=0, tiled=False) for x in kv_rot]
+        rest1 = [onward(x[:, :, group_size:]) for x in kv_rot]
+        rest2 = [onward(x) for x in rest1]
 
         def head_major(x):
             return jnp.transpose(x[0].reshape(seq_loc, kv_heads, group_size, head_dim), (1, 2, 0, 3))
 
         q_h, do_h = head_major(q_rope), head_major(d_out)
-        outs = [attention(a, n, shard, q_h, do_h, kv_rot, rest1, rest2, gathered[i]) for i, (a, n) in enumerate(zip(starts, CHUNKS))]
+        outs = [attention(a, n, shard, q_h, do_h, kv_rot[i], rest1[i], rest2[i], gathered[i]) for i, (a, n) in enumerate(zip(starts, CHUNKS))]
         reduced = [lax.psum_scatter(out[5], 'cp', scatter_dimension=0, tiled=False) for out in outs]
 
         def token_major(xs):

time: 482 us -> 471 us (0.977)
  waiting for transfers between devices: 193 us -> 161 us
  starting transfers between devices: 20.2 us -> 36.9 us
    reduce_scatter x3, waiting for transfers between devices: 153 us -> 118 us  [per_device(): lax.psum_scatter(out[5], 'cp', scatter_dimension=0, tiled=False)]
    ppermute x2 -> x6, starting transfers between devices: 9.05 us -> 26.3 us  [onward(): return lax.ppermute(x, 'cp', [(s, s + 1) for s in range(cp_size - 1)])]
    all_gather x3, waiting for transfers between devices: 2.43 us -> 13.5 us  [per_device(): lax.all_gather(x[:, :, :group_size], 'cp', axis=0, tiled=False)]
    ppermute x2 -> x6, waiting for transfers between devices: 36.1 us -> 29.2 us  [onward(): return lax.ppermute(x, 'cp', [(s, s + 1) for s in range(cp_size - 1)])]
    unnamed x32 -> x40, local copies, waits for them, and re-layouts: 24.6 us -> 26.1 us
  transfers between devices with their start and end apart: 14 -> 18, of which waited for: 5 -> 8; matrix products, arithmetic and copies ran while one was open for 6% -> 7% of each run, Pallas kernels for 42% -> 44%
where the time goes in v3:
time: 471 us; the launch traced here: 470 us
  Pallas kernels  213 us (45%)
  waiting for transfers between devices  161 us (34%)
  local copies, waits for them, and re-layouts  37.9 us (8%)
  starting transfers between devices  36.9 us (8%)
  between operations  14.4 us (3%)
  other arithmetic  6.84 us (1%)
    pallas_call x3, Pallas kernels, attention(): pl.pallas_call(attention_kernel, grid_spec=pltpu.PrefetchScalarGridSpec(n...  196 us
    reduce_scatter x3, waiting for transfers between devices, per_device(): lax.psum_scatter(out[5], 'cp', scatter_dimension=0, tiled=False)  118 us
    ppermute x6, waiting for transfers between devices, onward(): return lax.ppermute(x, 'cp', [(s, s + 1) for s in range(cp_size - 1)])  29.2 us
    ppermute x6, starting transfers between devices, onward(): return lax.ppermute(x, 'cp', [(s, s + 1) for s in range(cp_size - 1)])  26.3 us
    unnamed x40, local copies, waits for them, and re-layouts  26.1 us
    all_gather x3, waiting for transfers between devices, per_device(): lax.all_gather(x[:, :, :group_size], 'cp', axis=0, tiled=False)  13.5 us
    ppermute x6, starting transfers between devices, per_device(): lax.ppermute(out[2 + dist], 'cp', [(s + dist, s) for s in range(cp_size -...  10.3 us
  transfers between devices with their start and end apart: 18, of which 8 were waited for; matrix products, arithmetic and copies ran while one was open for 7% of the time, Pallas kernels for 44%

profile of v3, /device:TPU:21, one launch (start us, length us, event | category | flops | bytes accessed | tf_op | source)
XLA Modules:
  0.0 469.6 jit_solution(4791637218655874621)
XLA Ops:
  7.2 0.1 all-gather.7.cloned.1.call-start
  7.2 3.2 copy_bitcast_fusion
  10.5 1.8 rotate.3.ko_ref.vo_ref
  12.3 1.7 slice.32
  14.0 0.1 all-gather.7.cloned.1.call-update
  14.1 0.1 all-gather.9.cloned.1.call-start
  14.1 3.0 rotate.4.ko_ref.vo_ref
  17.1 1.9 slice.34
  19.0 0.1 all-gather.9.cloned.1.call-update
  19.0 0.1 all-gather.11.cloned.1.call-start
  19.1 2.9 rotate.5.ko_ref.vo_ref
  22.0 1.8 slice.36
  23.9 0.1 all-gather.11.cloned.1.call-update
  23.9 0.1 reduce-scatter.4.cloned.1.call-start
  24.0 1.1 slice.33
  25.1 5.2 %collective-permute-start = (bf16[2,2,3,64,128]{4,3,2,1,0:T(8,128)(2,1)S(1)}, bf16[2,2,3,64,128]{4,3,2,1,0:T(8,128)(2,1)S(1)}, u32[]{:S(2)}, u32[]{:S(2)}) collective-permute-start(bf16[2,2,3,64,128]{4,3,2,1,0:T(8,128)(2,1)S(1)} %slice.33), channel_id=1, source_target_pairs={{0,1},{1,2},{2,3},{3,4},{4,5},{5,6},{6,7},{7,8},{8,9},{9,10},{10,1... | collective-permute-start | bytes 589832 | tf_op jit(solution)/shard_map/ppermute | solution.py:355
  30.4 3.9 collective-permute-done.kr1_ref.vr1_ref
  34.3 4.4 collective-permute-start.1
  38.7 0.0 slice-start.1
  38.7 6.2 %copy.16 = bf16[1,512,40,128]{3,1,2,0:T(8,128)(2,1)} copy(bf16[1,512,40,128]{3,2,1,0:T(8,128)(2,1)} %param.4) | data formatting | bytes 10485760 | tf_op args[0]
  44.9 3.6 copy.17
  48.6 0.6 pad_add_fusion.info_ref
  49.1 13.5 %all-gather.7.cloned.1.call-done = bf16[32,2,5,64,128]{4,3,2,1,0:T(8,128)(2,1)} async-done(((bf16[2,2,5,64,128]{4,3,2,1,0:T(8,128)(2,1)}), bf16[32,2,5,64,128]{4,3,2,1,0:T(8,128)(2,1)}) %all-gather.7.cloned.1.call-update) | async-done | bytes 5242896 | tf_op jit(solution)/shard_map/all_gather | solution.py:358
  62.7 50.0 %attention.3 = (bf16[2,5,512,128]{3,2,1,0:T(8,128)(2,1)}, bf16[2,5,512,128]{3,2,1,0:T(8,128)(2,1)}, f32[2,2,8,64,128]{4,3,2,1,0:T(8,128)}, bf16[2,2,3,64,128]{4,...) custom-call(s32[2]{0:T(128)} %pad_add_fusion.info_ref, ...), custom_call_target="tpu_custom_call" | custom-call | flops 16609443840 | tf_op jit(solution)/shard_map/attention/pallas_call | solution.py:261
  112.7 0.1 reduce-scatter.4.cloned.1.call-update
  112.8 0.1 reduce-scatter.6.cloned.1.call-start
  112.8 1.0 slice.35
  113.8 2.9 collective-permute-start.2
  116.7 3.6 collective-permute-done.2.kr1_ref.vr1_ref
  120.3 4.6 collective-permute-start.3
  124.9 0.6 pad_add_fusion.1.info_ref
  125.6 8.9 %collective-permute-done.3.kr2_ref.vr2_ref = bf16[2,3,3,64,128]{4,3,2,1,0:T(8,128)(2,1)S(1)} collective-permute-done((bf16[2,3,3,64,128]{4,3,2,1,0:T(8,128)(2,1)S(1)}, bf16[2,3,3,64,128]{4,3,2,1,0:T(8,128)(2,1)S(1)}, u32[]{:S(2)}, u32[]{:S(2)}) %collective-permute-start.3) | collective-permute-done | bytes 294944 | tf_op jit(solution)/shard_map/ppermute | solution.py:355
  134.5 0.7 copy-done.12
  135.2 72.8 %attention.4 = (bf16[3,5,512,128]{3,2,1,0:T(8,128)(2,1)}, bf16[3,5,512,128]{3,2,1,0:T(8,128)(2,1)}, f32[2,3,8,64,128]{4,3,2,1,0:T(8,128)}, bf16[2,3,3,64,128]{4,...) custom-call(s32[2]{0:T(128)} %pad_add_fusion.1.info_ref, ...), custom_call_target="tpu_custom_call" | custom-call | flops 24914165760 | tf_op jit(solution)/shard_map/attention/pallas_call | solution.py:261
  208.0 0.1 reduce-scatter.6.cloned.1.call-update
  208.1 0.1 reduce-scatter.8.cloned.1.call-start
  208.2 1.0 slice.37
  209.2 4.5 collective-permute-start.4
  213.7 6.6 %collective-permute-done.4.kr1_ref.vr1_ref = bf16[2,3,3,64,128]{4,3,2,1,0:T(8,128)(2,1)S(1)} collective-permute-done((bf16[2,3,3,64,128]{4,3,2,1,0:T(8,128)(2,1)S(1)}, bf16[2,3,3,64,128]{4,3,2,1,0:T(8,128)(2,1)S(1)}, u32[]{:S(2)}, u32[]{:S(2)}) %collective-permute-start.4) | collective-permute-done | bytes 294944 | tf_op jit(solution)/shard_map/ppermute | solution.py:355
  220.3 4.6 collective-permute-start.5
  224.9 0.6 pad_add_fusion.2.info_ref
  225.5 6.2 %collective-permute-done.5.kr2_ref.vr2_ref = bf16[2,3,3,64,128]{4,3,2,1,0:T(8,128)(2,1)S(1)} collective-permute-done((bf16[2,3,3,64,128]{4,3,2,1,0:T(8,128)(2,1)S(1)}, bf16[2,3,3,64,128]{4,3,2,1,0:T(8,128)(2,1)S(1)}, u32[]{:S(2)}, u32[]{:S(2)}) %collective-permute-start.5) | collective-permute-done | bytes 294944 | tf_op jit(solution)/shard_map/ppermute | solution.py:355
  231.7 0.7 copy-done.11
  232.4 72.8 %attention.5 = (bf16[3,5,512,128]{3,2,1,0:T(8,128)(2,1)}, bf16[3,5,512,128]{3,2,1,0:T(8,128)(2,1)}, f32[2,3,8,64,128]{4,3,2,1,0:T(8,128)}, bf16[2,3,3,64,128]{4,...) custom-call(s32[2]{0:T(128)} %pad_add_fusion.2.info_ref, ...), custom_call_target="tpu_custom_call" | custom-call | flops 24914165760 | tf_op jit(solution)/shard_map/attention/pallas_call | solution.py:261
  305.3 0.1 reduce-scatter.8.cloned.1.call-update
  305.3 2.2 collective-permute-start.6
  307.6 1.3 collective-permute-start.7
  308.9 2.0 collective-permute-start.8
  310.8 1.3 collective-permute-start.9
  312.1 2.2 collective-permute-start.10
  314.3 2.7 pad_maximum_fusion.1
  317.1 5.7 %copy.21 = bf16[1,512,40,128]{3,2,1,0:T(8,128)(2,1)} copy(bf16[1,512,40,128]{3,1,2,0:T(8,128)(2,1)S(1)} %bitcast.29) | data formatting | bytes 10485760
  322.8 1.3 collective-permute-start.11
  324.1 0.8 pad_maximum_fusion
  324.9 5.7 %copy.20 = bf16[1,512,40,128]{3,2,1,0:T(8,128)(2,1)} copy(bf16[1,512,40,128]{3,1,2,0:T(8,128)(2,1)S(1)} %bitcast.30) | data formatting | bytes 10485760
  330.7 2.3 merge.3
  333.0 28.1 %reduce-scatter.6.cloned.1.call-done = f32[1,2,3,5,64,128]{5,4,3,2,1,0:T(8,128)} async-done(((f32[16,2,3,5,64,128]{5,4,3,2,1,0:T(8,128)}), f32[1,2,3,5,64,128]{5,4,3,2,1,0:T(8,128)}) %reduce-scatter.6.cloned.1.call-update) | async-done | bytes 983056 | tf_op jit(solution)/shard_map/reduce_scatter | solution.py:367
  361.1 3.5 merge.4
  364.6 89.7 %reduce-scatter.8.cloned.1.call-done = f32[1,2,3,5,64,128]{5,4,3,2,1,0:T(8,128)} async-done(((f32[16,2,3,5,64,128]{5,4,3,2,1,0:T(8,128)}), f32[1,2,3,5,64,128]{5,4,3,2,1,0:T(8,128)}) %reduce-scatter.8.cloned.1.call-update) | async-done | bytes 983056 | tf_op jit(solution)/shard_map/reduce_scatter | solution.py:367
  454.2 3.5 merge.5
  457.7 1.6 maximum_bitcast_fusion
  459.3 0.1 fusion
  459.5 1.6 copy.22
  461.1 1.6 copy.23
  (42 shorter events, 0.1 us)
Async XLA Ops:
  7.2 55.5 %all-gather.7.cloned.1.call-start = ((), (), s32[]{:S(2)}) async-start(), calls=%async_computation.6 | async-start | bytes 5570560 | tf_op jit(solution)/shard_map/all_gather | solution.py:358
  14.1 120.4 %all-gather.9.cloned.1.call-start = ((), (), s32[]{:S(2)}) async-start(), calls=%async_computation.7 | async-start | bytes 8355840 | tf_op jit(solution)/shard_map/all_gather | solution.py:358
  19.0 212.7 %all-gather.11.cloned.1.call-start = ((), (), s32[]{:S(2)}) async-start(), calls=%async_computation.8 | async-start | bytes 8355840 | tf_op jit(solution)/shard_map/all_gather | solution.py:358
  23.9 306.7 %reduce-scatter.4.cloned.1.call-start = ((), (), s32[]{:S(2)}) async-start(), calls=%async_computation.3 | async-start | bytes 11141120 | tf_op jit(solution)/shard_map/reduce_scatter | solution.py:367
  24.0 20.9 %slice-start = ((s8[5242880]{0:T(1024)(128)(4,1)}), s8[4194304]{0:T(1024)(128)(4,1)S(1)}, s32[]{:S(2)}) async-start(s8[5242880]{0:T(1024)(128)(4,1)} %bitcast.31), calls=%async_computation.9 | async-start | bytes 8388608
  25.1 9.2 %collective-permute-start = (bf16[2,2,3,64,128]{4,3,2,1,0:T(8,128)(2,1)S(1)}, bf16[2,2,3,64,128]{4,3,2,1,0:T(8,128)(2,1)S(1)}, u32[]{:S(2)}, u32[]{:S(2)}) collective-permute-start(bf16[2,2,3,64,128]{4,3,2,1,0:T(8,128)(2,1)S(1)} %slice.33), channel_id=1, source_target_pairs={{0,1},{1,2},{2,3},{3,4},{4,5},{5,6},{6,7},{7,8},{8,9},{9,10},{10,1... | collective-permute-start | bytes 589832 | tf_op jit(solution)/shard_map/ppermute | solution.py:355
  34.3 10.6 %copy-start.13 = (bf16[2,2,3,64,128]{4,3,2,1,0:T(8,128)(2,1)}, bf16[2,2,3,64,128]{4,3,2,1,0:T(8,128)(2,1)S(1)}, u32[]{:S(2)}) copy-start(bf16[2,2,3,64,128]{4,3,2,1,0:T(8,128)(2,1)S(1)} %collective-permute-done.kr1_ref.vr1_ref) | copy-start | bytes 589828
  34.3 14.9 %collective-permute-start.1 = (bf16[2,2,3,64,128]{4,3,2,1,0:T(8,128)(2,1)S(1)}, bf16[2,2,3,64,128]{4,3,2,1,0:T(8,128)(2,1)S(1)}, u32[]{:S(2)}, u32[]{:S(2)}) collective-permute-start(bf16[2,2,3,64,128]{4,3,2,1,0:T(8,128)(2,1)S(1)} %collective-permute-done.kr1_ref.vr1_ref), channel_id=1, source_target_pairs={{0,1},{1,2},{2,3},{3,4},{4,5},{5,6},{6,7},{7,8},{8,9},{9,10},{10,1... | collective-permute-start | bytes 589832 | tf_op jit(solution)/shard_map/ppermute | solution.py:355
  38.7 6.2 %slice-start.1 = ((s8[5242880]{0:T(1024)(128)(4,1)}), s8[1048576]{0:T(1024)(128)(4,1)S(1)}, s32[]{:S(2)}) async-start(s8[5242880]{0:T(1024)(128)(4,1)} %bitcast.31), calls=%async_computation.10 | async-start | bytes 2097152
  49.1 13.5 %copy-start.14 = (bf16[2,2,3,64,128]{4,3,2,1,0:T(8,128)(2,1)}, bf16[2,2,3,64,128]{4,3,2,1,0:T(8,128)(2,1)S(1)}, u32[]{:S(2)}) copy-start(bf16[2,2,3,64,128]{4,3,2,1,0:T(8,128)(2,1)S(1)} %collective-permute-done.1.kr2_ref.vr2_ref) | copy-start | bytes 589828
  112.8 248.3 %reduce-scatter.6.cloned.1.call-start = ((), (), s32[]{:S(2)}) async-start(), calls=%async_computation.4 | async-start | bytes 16711680 | tf_op jit(solution)/shard_map/reduce_scatter | solution.py:367
  113.8 6.5 %collective-permute-start.2 = (bf16[2,3,3,64,128]{4,3,2,1,0:T(8,128)(2,1)S(1)}, bf16[2,3,3,64,128]{4,3,2,1,0:T(8,128)(2,1)S(1)}, u32[]{:S(2)}, u32[]{:S(2)}) collective-permute-start(bf16[2,3,3,64,128]{4,3,2,1,0:T(8,128)(2,1)S(1)} %slice.35), channel_id=1, source_target_pairs={{0,1},{1,2},{2,3},{3,4},{4,5},{5,6},{6,7},{7,8},{8,9},{9,10},{10,1... | collective-permute-start | bytes 884744 | tf_op jit(solution)/shard_map/ppermute | solution.py:355
  120.3 14.2 %copy-start.10 = (bf16[2,3,3,64,128]{4,3,2,1,0:T(8,128)(2,1)}, bf16[2,3,3,64,128]{4,3,2,1,0:T(8,128)(2,1)S(1)}, u32[]{:S(2)}) copy-start(bf16[2,3,3,64,128]{4,3,2,1,0:T(8,128)(2,1)S(1)} %collective-permute-done.2.kr1_ref.vr1_ref) | copy-start | bytes 884740
  120.3 14.1 %collective-permute-start.3 = (bf16[2,3,3,64,128]{4,3,2,1,0:T(8,128)(2,1)S(1)}, bf16[2,3,3,64,128]{4,3,2,1,0:T(8,128)(2,1)S(1)}, u32[]{:S(2)}, u32[]{:S(2)}) collective-permute-start(bf16[2,3,3,64,128]{4,3,2,1,0:T(8,128)(2,1)S(1)} %collective-permute-done.2.kr1_ref.vr1_ref), channel_id=1, source_target_pairs={{0,1},{1,2},{2,3},{3,4},{4,5},{5,6},{6,7},{7,8},{8,9},{9,10},{10,1... | collective-permute-start | bytes 884744 | tf_op jit(solution)/shard_map/ppermute | solution.py:355
  134.5 0.7 copy-start.12
  208.1 246.2 %reduce-scatter.8.cloned.1.call-start = ((), (), s32[]{:S(2)}) async-start(), calls=%async_computation.5 | async-start | bytes 16711680 | tf_op jit(solution)/shard_map/reduce_scatter | solution.py:367
  209.2 11.1 %collective-permute-start.4 = (bf16[2,3,3,64,128]{4,3,2,1,0:T(8,128)(2,1)S(1)}, bf16[2,3,3,64,128]{4,3,2,1,0:T(8,128)(2,1)S(1)}, u32[]{:S(2)}, u32[]{:S(2)}) collective-permute-start(bf16[2,3,3,64,128]{4,3,2,1,0:T(8,128)(2,1)S(1)} %slice.37), channel_id=1, source_target_pairs={{0,1},{1,2},{2,3},{3,4},{4,5},{5,6},{6,7},{7,8},{8,9},{9,10},{10,1... | collective-permute-start | bytes 884744 | tf_op jit(solution)/shard_map/ppermute | solution.py:355
  220.3 11.4 %copy-start.9 = (bf16[2,3,3,64,128]{4,3,2,1,0:T(8,128)(2,1)}, bf16[2,3,3,64,128]{4,3,2,1,0:T(8,128)(2,1)S(1)}, u32[]{:S(2)}) copy-start(bf16[2,3,3,64,128]{4,3,2,1,0:T(8,128)(2,1)S(1)} %collective-permute-done.4.kr1_ref.vr1_ref) | copy-start | bytes 884740
  220.3 11.4 %collective-permute-start.5 = (bf16[2,3,3,64,128]{4,3,2,1,0:T(8,128)(2,1)S(1)}, bf16[2,3,3,64,128]{4,3,2,1,0:T(8,128)(2,1)S(1)}, u32[]{:S(2)}, u32[]{:S(2)}) collective-permute-start(bf16[2,3,3,64,128]{4,3,2,1,0:T(8,128)(2,1)S(1)} %collective-permute-done.4.kr1_ref.vr1_ref), channel_id=1, source_target_pairs={{0,1},{1,2},{2,3},{3,4},{4,5},{5,6},{6,7},{7,8},{8,9},{9,10},{10,1... | collective-permute-start | bytes 884744 | tf_op jit(solution)/shard_map/ppermute | solution.py:355
  231.7 0.7 copy-start.11
  305.3 9.1 %copy-start.2 = (bf16[3,5,512,128]{3,2,1,0:T(8,128)(2,1)S(1)}, bf16[3,5,512,128]{3,2,1,0:T(8,128)(2,1)}, u32[]{:S(2)}) copy-start(bf16[3,5,512,128]{3,2,1,0:T(8,128)(2,1)} %get-tuple-element.26) | copy-start | bytes 5898244
  305.3 9.1 %copy-start.5 = (bf16[2,5,512,128]{3,2,1,0:T(8,128)(2,1)S(1)}, bf16[2,5,512,128]{3,2,1,0:T(8,128)(2,1)}, u32[]{:S(2)}) copy-start(bf16[2,5,512,128]{3,2,1,0:T(8,128)(2,1)} %get-tuple-element.25) | copy-start | bytes 3932164
  305.3 17.5 %collective-permute-start.6 = (bf16[2,2,3,64,128]{4,3,2,1,0:T(8,128)(2,1)}, bf16[2,2,3,64,128]{4,3,2,1,0:T(8,128)(2,1)S(1)}, u32[]{:S(2)}, u32[]{:S(2)}) collective-permute-start(bf16[2,2,3,64,128]{4,3,2,1,0:T(8,128)(2,1)} %get-tuple-element.30), channel_id=1, source_target_pairs={{1,0},{2,1},{3,2},{4,3},{5,4},{6,5},{7,6},{8,7},{9,8},{10,9},{11,1... | collective-permute-start | bytes 589832 | tf_op jit(solution)/shard_map/ppermute | solution.py:378
  307.6 23.1 %collective-permute-start.7 = (bf16[2,2,3,64,128]{4,3,2,1,0:T(8,128)(2,1)}, bf16[2,2,3,64,128]{4,3,2,1,0:T(8,128)(2,1)}, u32[]{:S(2)}, u32[]{:S(2)}) collective-permute-start(bf16[2,2,3,64,128]{4,3,2,1,0:T(8,128)(2,1)} %get-tuple-element.31), channel_id=1, source_target_pairs={{2,0},{3,1},{4,2},{5,3},{6,4},{7,5},{8,6},{9,7},{10,8},{11,9},{12,... | collective-permute-start | bytes 589832 | tf_op jit(solution)/shard_map/ppermute | solution.py:378
  308.9 24.1 %collective-permute-start.8 = (bf16[2,3,3,64,128]{4,3,2,1,0:T(8,128)(2,1)}, bf16[2,3,3,64,128]{4,3,2,1,0:T(8,128)(2,1)}, u32[]{:S(2)}, u32[]{:S(2)}) collective-permute-start(bf16[2,3,3,64,128]{4,3,2,1,0:T(8,128)(2,1)} %get-tuple-element.34), channel_id=1, source_target_pairs={{1,0},{2,1},{3,2},{4,3},{5,4},{6,5},{7,6},{8,7},{9,8},{10,9},{11,1... | collective-permute-start | bytes 884744 | tf_op jit(solution)/shard_map/ppermute | solution.py:378
  310.8 22.1 %collective-permute-start.9 = (bf16[2,3,3,64,128]{4,3,2,1,0:T(8,128)(2,1)}, bf16[2,3,3,64,128]{4,3,2,1,0:T(8,128)(2,1)}, u32[]{:S(2)}, u32[]{:S(2)}) collective-permute-start(bf16[2,3,3,64,128]{4,3,2,1,0:T(8,128)(2,1)} %get-tuple-element.35), channel_id=1, source_target_pairs={{2,0},{3,1},{4,2},{5,3},{6,4},{7,5},{8,6},{9,7},{10,8},{11,9},{12,... | collective-permute-start | bytes 884744 | tf_op jit(solution)/shard_map/ppermute | solution.py:378
  312.1 52.4 %collective-permute-start.10 = (bf16[2,3,3,64,128]{4,3,2,1,0:T(8,128)(2,1)}, bf16[2,3,3,64,128]{4,3,2,1,0:T(8,128)(2,1)}, u32[]{:S(2)}, u32[]{:S(2)}) collective-permute-start(bf16[2,3,3,64,128]{4,3,2,1,0:T(8,128)(2,1)} %get-tuple-element.38), channel_id=1, source_target_pairs={{1,0},{2,1},{3,2},{4,3},{5,4},{6,5},{7,6},{8,7},{9,8},{10,9},{11,1... | collective-permute-start | bytes 884744 | tf_op jit(solution)/shard_map/ppermute | solution.py:378
  317.0 5.8 %copy-start.8 = (bf16[2,3,3,64,128]{4,3,2,1,0:T(8,128)(2,1)S(1)}, bf16[2,3,3,64,128]{4,3,2,1,0:T(8,128)(2,1)}, u32[]{:S(2)}) copy-start(bf16[2,3,3,64,128]{4,3,2,1,0:T(8,128)(2,1)} %get-tuple-element.39) | copy-start | bytes 884740
  317.0 7.1 %copy-start.1 = (bf16[3,5,512,128]{3,2,1,0:T(8,128)(2,1)S(1)}, bf16[3,5,512,128]{3,2,1,0:T(8,128)(2,1)}, u32[]{:S(2)}) copy-start(bf16[3,5,512,128]{3,2,1,0:T(8,128)(2,1)} %get-tuple-element.23) | copy-start | bytes 5898244
  317.0 7.1 %copy-start.3 = (bf16[3,5,512,128]{3,2,1,0:T(8,128)(2,1)S(1)}, bf16[3,5,512,128]{3,2,1,0:T(8,128)(2,1)}, u32[]{:S(2)}) copy-start(bf16[3,5,512,128]{3,2,1,0:T(8,128)(2,1)} %get-tuple-element.24) | copy-start | bytes 5898244
  317.1 7.1 %copy-start.4 = (bf16[2,5,512,128]{3,2,1,0:T(8,128)(2,1)S(1)}, bf16[2,5,512,128]{3,2,1,0:T(8,128)(2,1)}, u32[]{:S(2)}) copy-start(bf16[2,5,512,128]{3,2,1,0:T(8,128)(2,1)} %get-tuple-element.22) | copy-start | bytes 3932164
  322.8 2.1 copy-start.7
  322.8 41.8 %collective-permute-start.11 = (bf16[2,3,3,64,128]{4,3,2,1,0:T(8,128)(2,1)S(1)}, bf16[2,3,3,64,128]{4,3,2,1,0:T(8,128)(2,1)S(1)}, u32[]{:S(2)}, u32[]{:S(2)}) collective-permute-start(bf16[2,3,3,64,128]{4,3,2,1,0:T(8,128)(2,1)S(1)} %copy-done.8), channel_id=1, source_target_pairs={{2,0},{3,1},{4,2},{5,3},{6,4},{7,5},{8,6},{9,7},{10,8},{11,9},{12,... | collective-permute-start | bytes 884744 | tf_op jit(solution)/shard_map/ppermute | solution.py:378
  333.0 124.7 %copy-start = (bf16[2,2,512,128]{3,2,1,0:T(8,128)(2,1)S(1)}, bf16[2,2,512,128]{3,2,1,0:T(8,128)(2,1)}, u32[]{:S(2)}) copy-start(bf16[2,2,512,128]{3,2,1,0:T(8,128)(2,1)} %merge.3) | copy-start | bytes 1572868
  364.6 89.7 %copy-start.6 = (bf16[2,3,3,64,128]{4,3,2,1,0:T(8,128)(2,1)}, bf16[2,3,3,64,128]{4,3,2,1,0:T(8,128)(2,1)S(1)}, u32[]{:S(2)}) copy-start(bf16[2,3,3,64,128]{4,3,2,1,0:T(8,128)(2,1)S(1)} %collective-permute-done.11.back2_ref) | copy-start | bytes 884740
Sparse Core Ops, SparseCore 0:
  14.2 48.4 all-gather.6
  64.3 48.2 all-gather.8
  114.8 50.8 all-gather.10
  168.0 72.1 reduce-scatter.3
  242.3 118.7 reduce-scatter.5
  363.3 90.8 reduce-scatter.7

commit v4 on v3

--- a/solution.py
+++ b/solution.py
@@ -14,7 +14,7 @@
 ROWS = 256
 CHUNK = 128
 LOG2E = 1.4426950408889634
-CHUNKS = (2, 3, 3)
+CHUNKS = (3, 3, 2)
 F32 = jnp.float32
 BF16 = jnp.bfloat16
 

time: 471 us -> 471 us (level)
  no operation moved by 1% of the time
where the time goes in v4:
time: 471 us; the launch traced here: 469 us
  Pallas kernels  213 us (45%)
  waiting for transfers between devices  161 us (34%)
  local copies, waits for them, and re-layouts  37.9 us (8%)
  starting transfers between devices  36.9 us (8%)
  between operations  14.4 us (3%)
  other arithmetic  6.96 us (1%)
    pallas_call x3, Pallas kernels, attention(): pl.pallas_call(attention_kernel, grid_spec=pltpu.PrefetchScalarGridSpec(n...  196 us
    reduce_scatter x3, waiting for transfers between devices, per_device(): lax.psum_scatter(out[5], 'cp', scatter_dimension=0, tiled=False)  118 us
    ppermute x6, waiting for transfers between devices, onward(): return lax.ppermute(x, 'cp', [(s, s + 1) for s in range(cp_size - 1)])  29.2 us
    ppermute x6, starting transfers between devices, onward(): return lax.ppermute(x, 'cp', [(s, s + 1) for s in range(cp_size - 1)])  26.2 us
    unnamed x40, local copies, waits for them, and re-layouts  26.1 us
    all_gather x3, waiting for transfers between devices, per_device(): lax.all_gather(x[:, :, :group_size], 'cp', axis=0, tiled=False)  13.6 us
    ppermute x6, starting transfers between devices, per_device(): lax.ppermute(out[2 + dist], 'cp', [(s + dist, s) for s in range(cp_size -...  10.3 us
  transfers between devices with their start and end apart: 18, of which 8 were waited for; matrix products, arithmetic and copies ran while one was open for 7% of the time, Pallas kernels for 44%

profile of v4, /device:TPU:21, one launch (start us, length us, event | category | flops | bytes accessed | tf_op | source)
XLA Modules:
  0.0 469.5 jit_solution(10991135954932412151)
XLA Ops:
  7.2 0.1 all-gather.11.cloned.1.call-start
  7.2 3.2 copy_bitcast_fusion
  10.5 1.8 rotate.5.ko_ref.vo_ref
  12.3 1.7 slice.36
  14.0 0.1 all-gather.11.cloned.1.call-update
  14.1 0.1 all-gather.7.cloned.1.call-start
  14.1 2.9 rotate.3.ko_ref.vo_ref
  17.1 1.9 slice.32
  18.9 0.1 all-gather.7.cloned.1.call-update
  19.0 0.1 all-gather.9.cloned.1.call-start
  19.1 2.9 rotate.4.ko_ref.vo_ref
  22.0 1.8 slice.34
  23.9 0.1 all-gather.9.cloned.1.call-update
  23.9 0.1 reduce-scatter.8.cloned.1.call-start
  24.0 1.1 slice.37
  25.1 5.2 %collective-permute-start.4 = (bf16[2,2,3,64,128]{4,3,2,1,0:T(8,128)(2,1)S(1)}, bf16[2,2,3,64,128]{4,3,2,1,0:T(8,128)(2,1)S(1)}, u32[]{:S(2)}, u32[]{:S(2)}) collective-permute-start(bf16[2,2,3,64,128]{4,3,2,1,0:T(8,128)(2,1)S(1)} %slice.37), channel_id=1, source_target_pairs={{0,1},{1,2},{2,3},{3,4},{4,5},{5,6},{6,7},{7,8},{8,9},{9,10},{10,1... | collective-permute-start | bytes 589832 | tf_op jit(solution)/shard_map/ppermute | solution.py:355
  30.3 3.9 collective-permute-done.4.kr1_ref.vr1_ref
  34.2 4.4 collective-permute-start.5
  38.7 0.0 slice-start.1
  38.7 6.2 %copy.16 = bf16[1,512,40,128]{3,1,2,0:T(8,128)(2,1)} copy(bf16[1,512,40,128]{3,2,1,0:T(8,128)(2,1)} %param.4) | data formatting | bytes 10485760 | tf_op args[0]
  44.9 3.6 copy.17
  48.5 0.6 pad_add_fusion.2.info_ref
  49.1 13.6 %all-gather.11.cloned.1.call-done = bf16[32,2,5,64,128]{4,3,2,1,0:T(8,128)(2,1)} async-done(((bf16[2,2,5,64,128]{4,3,2,1,0:T(8,128)(2,1)}), bf16[32,2,5,64,128]{4,3,2,1,0:T(8,128)(2,1)}) %all-gather.11.cloned.1.call-update) | async-done | bytes 5242896 | tf_op jit(solution)/shard_map/all_gather | solution.py:358
  62.7 50.0 %attention.5 = (bf16[2,5,512,128]{3,2,1,0:T(8,128)(2,1)}, bf16[2,5,512,128]{3,2,1,0:T(8,128)(2,1)}, f32[2,2,8,64,128]{4,3,2,1,0:T(8,128)}, bf16[2,2,3,64,128]{4,...) custom-call(s32[2]{0:T(128)} %pad_add_fusion.2.info_ref, ...), custom_call_target="tpu_custom_call" | custom-call | flops 16609443840 | tf_op jit(solution)/shard_map/attention/pallas_call | solution.py:261
  112.7 0.1 reduce-scatter.8.cloned.1.call-update
  112.8 0.1 reduce-scatter.4.cloned.1.call-start
  112.9 1.0 slice.33
  113.8 2.8 collective-permute-start
  116.7 3.6 collective-permute-done.kr1_ref.vr1_ref
  120.3 4.6 collective-permute-start.1
  124.9 0.6 pad_add_fusion.info_ref
  125.5 8.9 %collective-permute-done.1.kr2_ref.vr2_ref = bf16[2,3,3,64,128]{4,3,2,1,0:T(8,128)(2,1)S(1)} collective-permute-done((bf16[2,3,3,64,128]{4,3,2,1,0:T(8,128)(2,1)S(1)}, bf16[2,3,3,64,128]{4,3,2,1,0:T(8,128)(2,1)S(1)}, u32[]{:S(2)}, u32[]{:S(2)}) %collective-permute-start.1) | collective-permute-done | bytes 294944 | tf_op jit(solution)/shard_map/ppermute | solution.py:355
  134.5 0.7 copy-done.12
  135.2 72.8 %attention.3 = (bf16[3,5,512,128]{3,2,1,0:T(8,128)(2,1)}, bf16[3,5,512,128]{3,2,1,0:T(8,128)(2,1)}, f32[2,3,8,64,128]{4,3,2,1,0:T(8,128)}, bf16[2,3,3,64,128]{4,...) custom-call(s32[2]{0:T(128)} %pad_add_fusion.info_ref, ...), custom_call_target="tpu_custom_call" | custom-call | flops 24914165760 | tf_op jit(solution)/shard_map/attention/pallas_call | solution.py:261
  208.0 0.1 reduce-scatter.4.cloned.1.call-update
  208.1 0.1 reduce-scatter.6.cloned.1.call-start
  208.2 1.0 slice.35
  209.2 4.5 collective-permute-start.2
  213.7 6.6 %collective-permute-done.2.kr1_ref.vr1_ref = bf16[2,3,3,64,128]{4,3,2,1,0:T(8,128)(2,1)S(1)} collective-permute-done((bf16[2,3,3,64,128]{4,3,2,1,0:T(8,128)(2,1)S(1)}, bf16[2,3,3,64,128]{4,3,2,1,0:T(8,128)(2,1)S(1)}, u32[]{:S(2)}, u32[]{:S(2)}) %collective-permute-start.2) | collective-permute-done | bytes 294944 | tf_op jit(solution)/shard_map/ppermute | solution.py:355
  220.3 4.6 collective-permute-start.3
  224.9 0.6 pad_add_fusion.1.info_ref
  225.5 6.2 %collective-permute-done.3.kr2_ref.vr2_ref = bf16[2,3,3,64,128]{4,3,2,1,0:T(8,128)(2,1)S(1)} collective-permute-done((bf16[2,3,3,64,128]{4,3,2,1,0:T(8,128)(2,1)S(1)}, bf16[2,3,3,64,128]{4,3,2,1,0:T(8,128)(2,1)S(1)}, u32[]{:S(2)}, u32[]{:S(2)}) %collective-permute-start.3) | collective-permute-done | bytes 294944 | tf_op jit(solution)/shard_map/ppermute | solution.py:355
  231.7 0.7 copy-done.11
  232.4 72.8 %attention.4 = (bf16[3,5,512,128]{3,2,1,0:T(8,128)(2,1)}, bf16[3,5,512,128]{3,2,1,0:T(8,128)(2,1)}, f32[2,3,8,64,128]{4,3,2,1,0:T(8,128)}, bf16[2,3,3,64,128]{4,...) custom-call(s32[2]{0:T(128)} %pad_add_fusion.1.info_ref, ...), custom_call_target="tpu_custom_call" | custom-call | flops 24914165760 | tf_op jit(solution)/shard_map/attention/pallas_call | solution.py:261
  305.3 0.1 reduce-scatter.6.cloned.1.call-update
  305.3 2.2 collective-permute-start.10
  307.6 1.3 collective-permute-start.11
  308.9 2.0 collective-permute-start.6
  310.8 1.3 collective-permute-start.7
  312.1 2.2 collective-permute-start.8
  314.3 2.7 pad_maximum_fusion.1
  317.1 5.7 %copy.21 = bf16[1,512,40,128]{3,2,1,0:T(8,128)(2,1)} copy(bf16[1,512,40,128]{3,1,2,0:T(8,128)(2,1)S(1)} %bitcast.29) | data formatting | bytes 10485760
  322.9 1.3 collective-permute-start.9
  324.2 0.8 pad_maximum_fusion
  325.0 5.7 %copy.20 = bf16[1,512,40,128]{3,2,1,0:T(8,128)(2,1)} copy(bf16[1,512,40,128]{3,1,2,0:T(8,128)(2,1)S(1)} %bitcast.30) | data formatting | bytes 10485760
  330.8 2.3 merge.5
  333.1 27.9 %reduce-scatter.4.cloned.1.call-done = f32[1,2,3,5,64,128]{5,4,3,2,1,0:T(8,128)} async-done(((f32[16,2,3,5,64,128]{5,4,3,2,1,0:T(8,128)}), f32[1,2,3,5,64,128]{5,4,3,2,1,0:T(8,128)}) %reduce-scatter.4.cloned.1.call-update) | async-done | bytes 983056 | tf_op jit(solution)/shard_map/reduce_scatter | solution.py:367
  360.9 3.5 merge.3
  364.4 89.7 %reduce-scatter.6.cloned.1.call-done = f32[1,2,3,5,64,128]{5,4,3,2,1,0:T(8,128)} async-done(((f32[16,2,3,5,64,128]{5,4,3,2,1,0:T(8,128)}), f32[1,2,3,5,64,128]{5,4,3,2,1,0:T(8,128)}) %reduce-scatter.6.cloned.1.call-update) | async-done | bytes 983056 | tf_op jit(solution)/shard_map/reduce_scatter | solution.py:367
  454.1 3.5 merge.4
  457.6 1.6 maximum_bitcast_fusion
  459.2 0.1 fusion
  459.3 1.6 copy.22
  461.0 1.6 copy.23
  (42 shorter events, 0.1 us)
Async XLA Ops:
  7.2 55.5 %all-gather.11.cloned.1.call-start = ((), (), s32[]{:S(2)}) async-start(), calls=%async_computation.8 | async-start | bytes 5570560 | tf_op jit(solution)/shard_map/all_gather | solution.py:358
  14.1 120.4 %all-gather.7.cloned.1.call-start = ((), (), s32[]{:S(2)}) async-start(), calls=%async_computation.6 | async-start | bytes 8355840 | tf_op jit(solution)/shard_map/all_gather | solution.py:358
  19.0 212.7 %all-gather.9.cloned.1.call-start = ((), (), s32[]{:S(2)}) async-start(), calls=%async_computation.7 | async-start | bytes 8355840 | tf_op jit(solution)/shard_map/all_gather | solution.py:358
  23.9 306.9 %reduce-scatter.8.cloned.1.call-start = ((), (), s32[]{:S(2)}) async-start(), calls=%async_computation.5 | async-start | bytes 11141120 | tf_op jit(solution)/shard_map/reduce_scatter | solution.py:367
  24.0 20.9 %slice-start = ((s8[5242880]{0:T(1024)(128)(4,1)}), s8[4194304]{0:T(1024)(128)(4,1)S(1)}, s32[]{:S(2)}) async-start(s8[5242880]{0:T(1024)(128)(4,1)} %bitcast.31), calls=%async_computation.9 | async-start | bytes 8388608
  25.1 9.1 %collective-permute-start.4 = (bf16[2,2,3,64,128]{4,3,2,1,0:T(8,128)(2,1)S(1)}, bf16[2,2,3,64,128]{4,3,2,1,0:T(8,128)(2,1)S(1)}, u32[]{:S(2)}, u32[]{:S(2)}) collective-permute-start(bf16[2,2,3,64,128]{4,3,2,1,0:T(8,128)(2,1)S(1)} %slice.37), channel_id=1, source_target_pairs={{0,1},{1,2},{2,3},{3,4},{4,5},{5,6},{6,7},{7,8},{8,9},{9,10},{10,1... | collective-permute-start | bytes 589832 | tf_op jit(solution)/shard_map/ppermute | solution.py:355
  34.2 10.6 %copy-start.13 = (bf16[2,2,3,64,128]{4,3,2,1,0:T(8,128)(2,1)}, bf16[2,2,3,64,128]{4,3,2,1,0:T(8,128)(2,1)S(1)}, u32[]{:S(2)}) copy-start(bf16[2,2,3,64,128]{4,3,2,1,0:T(8,128)(2,1)S(1)} %collective-permute-done.4.kr1_ref.vr1_ref) | copy-start | bytes 589828
  34.2 14.9 %collective-permute-start.5 = (bf16[2,2,3,64,128]{4,3,2,1,0:T(8,128)(2,1)S(1)}, bf16[2,2,3,64,128]{4,3,2,1,0:T(8,128)(2,1)S(1)}, u32[]{:S(2)}, u32[]{:S(2)}) collective-permute-start(bf16[2,2,3,64,128]{4,3,2,1,0:T(8,128)(2,1)S(1)} %collective-permute-done.4.kr1_ref.vr1_ref), channel_id=1, source_target_pairs={{0,1},{1,2},{2,3},{3,4},{4,5},{5,6},{6,7},{7,8},{8,9},{9,10},{10,1... | collective-permute-start | bytes 589832 | tf_op jit(solution)/shard_map/ppermute | solution.py:355
  38.7 6.2 %slice-start.1 = ((s8[5242880]{0:T(1024)(128)(4,1)}), s8[1048576]{0:T(1024)(128)(4,1)S(1)}, s32[]{:S(2)}) async-start(s8[5242880]{0:T(1024)(128)(4,1)} %bitcast.31), calls=%async_computation.10 | async-start | bytes 2097152
  49.1 13.6 %copy-start.14 = (bf16[2,2,3,64,128]{4,3,2,1,0:T(8,128)(2,1)}, bf16[2,2,3,64,128]{4,3,2,1,0:T(8,128)(2,1)S(1)}, u32[]{:S(2)}) copy-start(bf16[2,2,3,64,128]{4,3,2,1,0:T(8,128)(2,1)S(1)} %collective-permute-done.5.kr2_ref.vr2_ref) | copy-start | bytes 589828
  112.8 248.2 %reduce-scatter.4.cloned.1.call-start = ((), (), s32[]{:S(2)}) async-start(), calls=%async_computation.3 | async-start | bytes 16711680 | tf_op jit(solution)/shard_map/reduce_scatter | solution.py:367
  113.8 6.5 %collective-permute-start = (bf16[2,3,3,64,128]{4,3,2,1,0:T(8,128)(2,1)S(1)}, bf16[2,3,3,64,128]{4,3,2,1,0:T(8,128)(2,1)S(1)}, u32[]{:S(2)}, u32[]{:S(2)}) collective-permute-start(bf16[2,3,3,64,128]{4,3,2,1,0:T(8,128)(2,1)S(1)} %slice.33), channel_id=1, source_target_pairs={{0,1},{1,2},{2,3},{3,4},{4,5},{5,6},{6,7},{7,8},{8,9},{9,10},{10,1... | collective-permute-start | bytes 884744 | tf_op jit(solution)/shard_map/ppermute | solution.py:355
  120.3 14.2 %copy-start.10 = (bf16[2,3,3,64,128]{4,3,2,1,0:T(8,128)(2,1)}, bf16[2,3,3,64,128]{4,3,2,1,0:T(8,128)(2,1)S(1)}, u32[]{:S(2)}) copy-start(bf16[2,3,3,64,128]{4,3,2,1,0:T(8,128)(2,1)S(1)} %collective-permute-done.kr1_ref.vr1_ref) | copy-start | bytes 884740
  120.3 14.2 %collective-permute-start.1 = (bf16[2,3,3,64,128]{4,3,2,1,0:T(8,128)(2,1)S(1)}, bf16[2,3,3,64,128]{4,3,2,1,0:T(8,128)(2,1)S(1)}, u32[]{:S(2)}, u32[]{:S(2)}) collective-permute-start(bf16[2,3,3,64,128]{4,3,2,1,0:T(8,128)(2,1)S(1)} %collective-permute-done.kr1_ref.vr1_ref), channel_id=1, source_target_pairs={{0,1},{1,2},{2,3},{3,4},{4,5},{5,6},{6,7},{7,8},{8,9},{9,10},{10,1... | collective-permute-start | bytes 884744 | tf_op jit(solution)/shard_map/ppermute | solution.py:355
  134.5 0.7 copy-start.12
  208.1 246.0 %reduce-scatter.6.cloned.1.call-start = ((), (), s32[]{:S(2)}) async-start(), calls=%async_computation.4 | async-start | bytes 16711680 | tf_op jit(solution)/shard_map/reduce_scatter | solution.py:367
  209.2 11.1 %collective-permute-start.2 = (bf16[2,3,3,64,128]{4,3,2,1,0:T(8,128)(2,1)S(1)}, bf16[2,3,3,64,128]{4,3,2,1,0:T(8,128)(2,1)S(1)}, u32[]{:S(2)}, u32[]{:S(2)}) collective-permute-start(bf16[2,3,3,64,128]{4,3,2,1,0:T(8,128)(2,1)S(1)} %slice.35), channel_id=1, source_target_pairs={{0,1},{1,2},{2,3},{3,4},{4,5},{5,6},{6,7},{7,8},{8,9},{9,10},{10,1... | collective-permute-start | bytes 884744 | tf_op jit(solution)/shard_map/ppermute | solution.py:355
  220.3 11.4 %copy-start.9 = (bf16[2,3,3,64,128]{4,3,2,1,0:T(8,128)(2,1)}, bf16[2,3,3,64,128]{4,3,2,1,0:T(8,128)(2,1)S(1)}, u32[]{:S(2)}) copy-start(bf16[2,3,3,64,128]{4,3,2,1,0:T(8,128)(2,1)S(1)} %collective-permute-done.2.kr1_ref.vr1_ref) | copy-start | bytes 884740
  220.3 11.4 %collective-permute-start.3 = (bf16[2,3,3,64,128]{4,3,2,1,0:T(8,128)(2,1)S(1)}, bf16[2,3,3,64,128]{4,3,2,1,0:T(8,128)(2,1)S(1)}, u32[]{:S(2)}, u32[]{:S(2)}) collective-permute-start(bf16[2,3,3,64,128]{4,3,2,1,0:T(8,128)(2,1)S(1)} %collective-permute-done.2.kr1_ref.vr1_ref), channel_id=1, source_target_pairs={{0,1},{1,2},{2,3},{3,4},{4,5},{5,6},{6,7},{7,8},{8,9},{9,10},{10,1... | collective-permute-start | bytes 884744 | tf_op jit(solution)/shard_map/ppermute | solution.py:355
  231.7 0.7 copy-start.11
  305.3 9.1 %copy-start.2 = (bf16[3,5,512,128]{3,2,1,0:T(8,128)(2,1)S(1)}, bf16[3,5,512,128]{3,2,1,0:T(8,128)(2,1)}, u32[]{:S(2)}) copy-start(bf16[3,5,512,128]{3,2,1,0:T(8,128)(2,1)} %get-tuple-element.25) | copy-start | bytes 5898244
  305.3 9.1 %copy-start.5 = (bf16[2,5,512,128]{3,2,1,0:T(8,128)(2,1)S(1)}, bf16[2,5,512,128]{3,2,1,0:T(8,128)(2,1)}, u32[]{:S(2)}) copy-start(bf16[2,5,512,128]{3,2,1,0:T(8,128)(2,1)} %get-tuple-element.27) | copy-start | bytes 3932164
  305.3 17.5 %collective-permute-start.10 = (bf16[2,2,3,64,128]{4,3,2,1,0:T(8,128)(2,1)}, bf16[2,2,3,64,128]{4,3,2,1,0:T(8,128)(2,1)S(1)}, u32[]{:S(2)}, u32[]{:S(2)}) collective-permute-start(bf16[2,2,3,64,128]{4,3,2,1,0:T(8,128)(2,1)} %get-tuple-element.38), channel_id=1, source_target_pairs={{1,0},{2,1},{3,2},{4,3},{5,4},{6,5},{7,6},{8,7},{9,8},{10,9},{11,1... | collective-permute-start | bytes 589832 | tf_op jit(solution)/shard_map/ppermute | solution.py:378
  307.6 23.2 %collective-permute-start.11 = (bf16[2,2,3,64,128]{4,3,2,1,0:T(8,128)(2,1)}, bf16[2,2,3,64,128]{4,3,2,1,0:T(8,128)(2,1)}, u32[]{:S(2)}, u32[]{:S(2)}) collective-permute-start(bf16[2,2,3,64,128]{4,3,2,1,0:T(8,128)(2,1)} %get-tuple-element.39), channel_id=1, source_target_pairs={{2,0},{3,1},{4,2},{5,3},{6,4},{7,5},{8,6},{9,7},{10,8},{11,9},{12,... | collective-permute-start | bytes 589832 | tf_op jit(solution)/shard_map/ppermute | solution.py:378
  308.9 24.2 %collective-permute-start.6 = (bf16[2,3,3,64,128]{4,3,2,1,0:T(8,128)(2,1)}, bf16[2,3,3,64,128]{4,3,2,1,0:T(8,128)(2,1)}, u32[]{:S(2)}, u32[]{:S(2)}) collective-permute-start(bf16[2,3,3,64,128]{4,3,2,1,0:T(8,128)(2,1)} %get-tuple-element.30), channel_id=1, source_target_pairs={{1,0},{2,1},{3,2},{4,3},{5,4},{6,5},{7,6},{8,7},{9,8},{10,9},{11,1... | collective-permute-start | bytes 884744 | tf_op jit(solution)/shard_map/ppermute | solution.py:378
  310.8 22.3 %collective-permute-start.7 = (bf16[2,3,3,64,128]{4,3,2,1,0:T(8,128)(2,1)}, bf16[2,3,3,64,128]{4,3,2,1,0:T(8,128)(2,1)}, u32[]{:S(2)}, u32[]{:S(2)}) collective-permute-start(bf16[2,3,3,64,128]{4,3,2,1,0:T(8,128)(2,1)} %get-tuple-element.31), channel_id=1, source_target_pairs={{2,0},{3,1},{4,2},{5,3},{6,4},{7,5},{8,6},{9,7},{10,8},{11,9},{12,... | collective-permute-start | bytes 884744 | tf_op jit(solution)/shard_map/ppermute | solution.py:378
  312.1 52.3 %collective-permute-start.8 = (bf16[2,3,3,64,128]{4,3,2,1,0:T(8,128)(2,1)}, bf16[2,3,3,64,128]{4,3,2,1,0:T(8,128)(2,1)}, u32[]{:S(2)}, u32[]{:S(2)}) collective-permute-start(bf16[2,3,3,64,128]{4,3,2,1,0:T(8,128)(2,1)} %get-tuple-element.34), channel_id=1, source_target_pairs={{1,0},{2,1},{3,2},{4,3},{5,4},{6,5},{7,6},{8,7},{9,8},{10,9},{11,1... | collective-permute-start | bytes 884744 | tf_op jit(solution)/shard_map/ppermute | solution.py:378
  317.1 5.8 %copy-start.8 = (bf16[2,3,3,64,128]{4,3,2,1,0:T(8,128)(2,1)S(1)}, bf16[2,3,3,64,128]{4,3,2,1,0:T(8,128)(2,1)}, u32[]{:S(2)}) copy-start(bf16[2,3,3,64,128]{4,3,2,1,0:T(8,128)(2,1)} %get-tuple-element.35) | copy-start | bytes 884740
  317.1 7.1 %copy-start.1 = (bf16[3,5,512,128]{3,2,1,0:T(8,128)(2,1)S(1)}, bf16[3,5,512,128]{3,2,1,0:T(8,128)(2,1)}, u32[]{:S(2)}) copy-start(bf16[3,5,512,128]{3,2,1,0:T(8,128)(2,1)} %get-tuple-element.22) | copy-start | bytes 5898244
  317.1 7.1 %copy-start.3 = (bf16[3,5,512,128]{3,2,1,0:T(8,128)(2,1)S(1)}, bf16[3,5,512,128]{3,2,1,0:T(8,128)(2,1)}, u32[]{:S(2)}) copy-start(bf16[3,5,512,128]{3,2,1,0:T(8,128)(2,1)} %get-tuple-element.23) | copy-start | bytes 5898244
  317.1 7.1 %copy-start.4 = (bf16[2,5,512,128]{3,2,1,0:T(8,128)(2,1)S(1)}, bf16[2,5,512,128]{3,2,1,0:T(8,128)(2,1)}, u32[]{:S(2)}) copy-start(bf16[2,5,512,128]{3,2,1,0:T(8,128)(2,1)} %get-tuple-element.24) | copy-start | bytes 3932164
  322.8 2.2 copy-start.7
  322.9 41.6 %collective-permute-start.9 = (bf16[2,3,3,64,128]{4,3,2,1,0:T(8,128)(2,1)S(1)}, bf16[2,3,3,64,128]{4,3,2,1,0:T(8,128)(2,1)S(1)}, u32[]{:S(2)}, u32[]{:S(2)}) collective-permute-start(bf16[2,3,3,64,128]{4,3,2,1,0:T(8,128)(2,1)S(1)} %copy-done.8), channel_id=1, source_target_pairs={{2,0},{3,1},{4,2},{5,3},{6,4},{7,5},{8,6},{9,7},{10,8},{11,9},{12,... | collective-permute-start | bytes 884744 | tf_op jit(solution)/shard_map/ppermute | solution.py:378
  333.1 124.5 %copy-start = (bf16[2,2,512,128]{3,2,1,0:T(8,128)(2,1)S(1)}, bf16[2,2,512,128]{3,2,1,0:T(8,128)(2,1)}, u32[]{:S(2)}) copy-start(bf16[2,2,512,128]{3,2,1,0:T(8,128)(2,1)} %merge.5) | copy-start | bytes 1572868
  364.4 89.7 %copy-start.6 = (bf16[2,3,3,64,128]{4,3,2,1,0:T(8,128)(2,1)}, bf16[2,3,3,64,128]{4,3,2,1,0:T(8,128)(2,1)S(1)}, u32[]{:S(2)}) copy-start(bf16[2,3,3,64,128]{4,3,2,1,0:T(8,128)(2,1)S(1)} %collective-permute-done.9.back2_ref) | copy-start | bytes 884740
Sparse Core Ops, SparseCore 0:
  14.2 48.4 all-gather.10
  64.3 48.2 all-gather.6
  114.8 50.9 all-gather.8
  168.0 72.1 reduce-scatter.7
  242.3 118.5 reduce-scatter.3
  363.2 90.8 reduce-scatter.5
